TPU v7x, 32 devices: a 4x4x1 block of a 4x4x8 slice. The times are simulated.
32 devices in a mesh: rep: 1 (over z), data: 4 (over y), model: 8 (over x, core).
Axes of the slice: x: 4, y: 4, z: 1, core: 2. Of those that a mesh axis runs over, the one named last changes fastest.
The devices are a block of a 4x4x8 slice.
Arguments:
- x: bfloat16 [32, 1024, 2048], P(('rep', 'data'), 'model')
- lengths: int32 [32], P(('rep', 'data'))
- gamma: bfloat16 [2, 2048], P(None, 'data')
- w_in: bfloat16 [2, 2048, 18432], P(None, 'data', 'model')
- w_kv: bfloat16 [2, 2048, 256], P(None, 'data')
- w_out: bfloat16 [2, 10240, 2048], P(None, 'model', 'data')
Outputs:
- output: bfloat16 [32, 1024, 2048], P(('rep', 'data'), 'model')
All inputs are finite; a program needn't handle non-finite values.
Results may differ from a plain program's by a relative error of at most 0.0158209.
Values are sent between devices in bfloat16 or wider.
A program may use at most 768 MiB of HBM per device.

v0:
```python
import jax
import jax.numpy as jnp
from jax import lax
from jax.sharding import PartitionSpec as P

EPSILON = 1e-6


def rms_norm(x_in, gain):
    x_f32 = x_in.astype(jnp.float32)
    inv_rms = lax.rsqrt(jnp.mean(x_f32 * x_f32, axis=-1, keepdims=True) + EPSILON)
    return (x_f32 * inv_rms * gain.astype(jnp.float32)).astype(jnp.bfloat16)


def attend(queries, keys, values, seq_lens, q_offset, block_len):
    n_batch, n_query, n_heads, head_dim = queries.shape
    n_blocks = n_query // block_len
    q_blocks = queries.reshape(n_batch, n_blocks, block_len, n_heads, head_dim)
    key_pos = jnp.arange(keys.shape[1])

    def one_block(blk_idx):
        q_blk = lax.dynamic_index_in_dim(q_blocks, blk_idx, axis=1, keepdims=False)
        scores = jnp.einsum("crie,cle->cirl", q_blk, keys, preferred_element_type=jnp.float32) * (head_dim ** -0.5)
        q_pos = q_offset + blk_idx * block_len + jnp.arange(block_len)
        visible = (key_pos[None, None, :] <= q_pos[None, :, None]) & (key_pos[None, None, :] < seq_lens[:, None, None])
        scores = jnp.where(visible[:, None], scores, -1e30)
        attn_probs = jax.nn.softmax(scores, axis=-1).astype(jnp.bfloat16)
        blk_out = jnp.einsum("cirl,cle->crie", attn_probs, values, preferred_element_type=jnp.float32)
        return blk_out.astype(jnp.bfloat16).reshape(n_batch, block_len, n_heads * head_dim)

    return lax.map(one_block, jnp.arange(n_blocks))


def solution(mesh):
    batch_axes = ("rep", "data")

    def local_step(x_loc, lens_loc, gamma_loc, w_in_loc, w_kv_loc, w_out_loc):
        n_batch, seq_loc, d_model = x_loc.shape
        head_dim = w_kv_loc.shape[2] // 2
        in_local = w_in_loc.shape[2]
        out_local = w_out_loc.shape[1]
        ff_local = in_local - out_local
        attn_cols = out_local - ff_local
        hidden = x_loc
        for layer in range(gamma_loc.shape[0]):
            gain = lax.all_gather(gamma_loc[layer], "data", axis=0, tiled=True)
            w_in_full = lax.all_gather(w_in_loc[layer], "data", axis=0, tiled=True)
            w_kv_full = lax.all_gather(w_kv_loc[layer], "data", axis=0, tiled=True)
            w_out_full = lax.all_gather(w_out_loc[layer], "data", axis=1, tiled=True)
            normed = rms_norm(hidden, gain)
            h_full = lax.all_gather(normed, "model", axis=1, tiled=True)
            seq_len = h_full.shape[1]
            projected = jnp.einsum("btd,dc->btc", h_full, w_in_full, preferred_element_type=jnp.float32).astype(jnp.bfloat16)
            key_value = jnp.einsum("btd,de->bte", h_full, w_kv_full, preferred_element_type=jnp.float32).astype(jnp.bfloat16)
            queries = projected[:, :, :attn_cols].reshape(n_batch, seq_len, attn_cols // head_dim, head_dim)
            attn_blocks = attend(queries, key_value[:, :, :head_dim], key_value[:, :, head_dim:], lens_loc, 0, seq_loc)
            gate = projected[:, :, attn_cols:attn_cols + ff_local].astype(jnp.float32)
            up_proj = projected[:, :, attn_cols + ff_local:].astype(jnp.float32)
            mlp_out = (jax.nn.silu(gate) * up_proj).astype(jnp.bfloat16)
            z_attn = jnp.einsum("nbqe,ed->bnqd", attn_blocks, w_out_full[:attn_cols], preferred_element_type=jnp.float32).reshape(n_batch, seq_len, d_model)
            z_mlp = jnp.einsum("btf,fd->btd", mlp_out, w_out_full[attn_cols:], preferred_element_type=jnp.float32)
            z_part = (z_attn + z_mlp).astype(jnp.bfloat16)
            z_sum = lax.psum_scatter(z_part, "model", scatter_dimension=1, tiled=True)
            hidden = (hidden.astype(jnp.float32) + z_sum.astype(jnp.float32)).astype(jnp.bfloat16)
        return hidden

    in_specs = (
        P(batch_axes, "model", None),
        P(batch_axes),
        P(None, "data"),
        P(None, "data", "model"),
        P(None, "data", None),
        P(None, "model", "data"),
    )
    return jax.shard_map(local_step, mesh=mesh, in_specs=in_specs, out_specs=P(batch_axes, "model", None), check_vma=False)
```

profile of v0, /device:TPU:97, one launch (start us, length us, event | category | flops | bytes accessed | tf_op | source)
XLA Modules:
  0.0 1811.8 jit_solution(7546421952167883599)
XLA Ops:
  6.6 4.8 fusion.74
  12.1 11.6 all-gather
  26.9 5.2 fusion.62
  35.2 69.7 %all-gather.21.cloned.1.call-done = bf16[1,2048,2304]{2,1,0:T(8,128)(2,1)} async-done(((bf16[1,512,2304]{2,1,0:T(8,128)(2,1)}), bf16[1,2048,2304]{2,1,0:T(8,128)(2,1)}) %all-gather.21.cloned.1.call-update) | async-done | bytes 9437200 | tf_op jit(solution)/shard_map/all_gather | solution.py:47
  104.9 157.4 %all-gather.17.cloned.1.call-done = bf16[8,1024,2048]{2,1,0:T(8,128)(2,1)} async-done(((bf16[8,128,2048]{2,1,0:T(8,128)(2,1)}), bf16[8,1024,2048]{2,1,0:T(8,128)(2,1)}) %all-gather.17.cloned.1.call-update) | async-done | bytes 33554448 | tf_op jit(solution)/shard_map/all_gather | solution.py:51
  262.3 86.4 %convolution_convert_fusion.1 = bf16[8,1024,2304]{2,1,0:T(8,128)(2,1)} fusion(bf16[8,1024,2048]{2,1,0:T(8,128)(2,1)} %all-gather.17.cloned.1.call-done, bf16[1,2048,2304]{2,1,0:T(8,128)(2,1)} %all-gather.21.cloned.1.call-done), kind=kOutput, calls=%fused_computation.69 | convolution fusion | flops 77328285696 | bytes 80740352 | tf_op jit(solution)/shard_map/btd,dc->btc/dot_general | solution.py:53
  348.8 4.6 slice.92
  353.3 6.9 reshape_reshape.6
  360.3 15.6 convolution_convert_fusion.3
  385.3 228.2 %while.24 = (s32[]{:T(128)}, bf16[8,8,128,256]{2,3,1,0:T(8,128)(2,1)}, s32[8]{0:T(128)S(1)}, s32[8]{0:T(128)S(1)}, bf16[8,8,128,2,128]{4,3,2,1,0:T(2,128)(2,1)},...) while((s32[]{:T(128)}, ...), condition=%wide.region_4.5_spmd.clone.clone, body=%wide.region_1.4_spmd.clone.clone.sunk | while | flops 1091970176 | bytes 51676904 | solution.py:31
  389.1 4.5 fusion.101
  395.0 12.8 fusion.102
  407.9 5.1 fusion.103
  423.6 12.8 fusion.102
  436.4 5.1 fusion.103
  446.2 4.5 fusion.101
  452.1 12.8 fusion.102
  464.9 5.1 fusion.103
  474.7 4.5 fusion.101
  480.6 12.8 fusion.102
  493.4 5.1 fusion.103
  509.1 12.8 fusion.102
  522.0 5.1 fusion.103
  531.8 4.5 fusion.101
  537.6 12.8 fusion.102
  550.5 5.1 fusion.103
  566.2 12.8 fusion.102
  579.0 5.1 fusion.103
  594.7 12.8 fusion.102
  607.5 5.1 fusion.103
  613.5 25.4 %convolution_bitcast_fusion.1 = f32[8,8,128,2048]{3,2,0,1:T(8,128)} fusion(bf16[8,8,128,256]{2,3,1,0:T(8,128)(2,1)} %get-tuple-element.95, bf16[1,1280,2048]{2,1,0:T(8,128)(2,1)} %all-gather.25.cloned.1.call-done), kind=kOutput, calls=%fused_computation.71 | convolution fusion | flops 8589934592 | bytes 72351744 | tf_op jit(solution)/shard_map/nbqe,ed->bnqd/dot_general | solution.py:60
  638.8 44.8 %copy.10 = f32[8,8,128,2048]{3,2,1,0:T(8,128)} copy(f32[8,8,128,2048]{3,2,0,1:T(8,128)} %convolution_bitcast_fusion.1) | data formatting | bytes 134217728 | tf_op jit(solution)/shard_map/nbqe,ed->bnqd/transpose | solution.py:60
  683.6 53.7 %fusion.39 = bf16[8,1024,2048]{2,1,0:T(8,128)(2,1)} fusion(f32[8,8,128,2048]{3,2,1,0:T(8,128)} %copy.10, bf16[8,1024,2304]{2,1,0:T(8,128)(2,1)} %convolution_convert_fusion.1, bf16[1,1280,2048]{2,1,0:T(8,128)(2,1)} %all-gather.25.cloned.1.call-done), kind=kOutput, calls=%fused_computation.53 | convolution fusion | flops 34460401664 | bytes 138412032 | tf_op jit(solution)/shard_map/btf,fd->btd/dot_general | solution.py:61
  738.0 9.7 all-gather.4
  747.7 157.7 %reduce-scatter.3.cloned.1.call-done = bf16[8,128,2048]{2,1,0:T(8,128)(2,1)} async-done(((bf16[8,1024,2048]{2,1,0:T(8,128)(2,1)}), bf16[8,128,2048]{2,1,0:T(8,128)(2,1)}) %reduce-scatter.3.cloned.1.call-update) | async-done | bytes 4194320 | tf_op jit(solution)/shard_map/reduce_scatter | solution.py:63
  905.5 5.0 fusion.64
  916.7 79.8 %all-gather.27.cloned.1.call-done = bf16[1,2048,2304]{2,1,0:T(8,128)(2,1)} async-done(((bf16[1,512,2304]{2,1,0:T(8,128)(2,1)}), bf16[1,2048,2304]{2,1,0:T(8,128)(2,1)}) %all-gather.27.cloned.1.call-update) | async-done | bytes 9437200 | tf_op jit(solution)/shard_map/all_gather | solution.py:47
  996.5 157.4 %all-gather.19.cloned.1.call-done = bf16[8,1024,2048]{2,1,0:T(8,128)(2,1)} async-done(((bf16[8,128,2048]{2,1,0:T(8,128)(2,1)}), bf16[8,1024,2048]{2,1,0:T(8,128)(2,1)}) %all-gather.19.cloned.1.call-update) | async-done | bytes 33554448 | tf_op jit(solution)/shard_map/all_gather | solution.py:51
  1153.9 86.6 %convolution_convert_fusion = bf16[8,1024,2304]{2,1,0:T(8,128)(2,1)} fusion(bf16[8,1024,2048]{2,1,0:T(8,128)(2,1)} %all-gather.19.cloned.1.call-done, bf16[1,2048,2304]{2,1,0:T(8,128)(2,1)} %all-gather.27.cloned.1.call-done), kind=kOutput, calls=%fused_computation.68 | convolution fusion | flops 77328285696 | bytes 80740352 | tf_op jit(solution)/shard_map/btd,dc->btc/dot_general | solution.py:53
  1240.5 4.6 slice.99
  1245.1 6.9 reshape_reshape.7
  1252.0 15.6 convolution_convert_fusion.2
  1277.0 225.7 %while.25 = (s32[]{:T(128)}, bf16[8,8,128,256]{2,3,1,0:T(8,128)(2,1)}, s32[8]{0:T(128)S(1)}, s32[8]{0:T(128)S(1)}, bf16[8,8,128,2,128]{4,3,2,1,0:T(2,128)(2,1)},...) while((s32[]{:T(128)}, ...), condition=%wide.region_10.11_spmd.clone.clone, body=%wide.region_7.10_spmd.clone.clone.sunk | while | flops 1091970176 | bytes 51676904 | solution.py:31
  1286.4 12.8 fusion.107
  1299.3 5.1 fusion.108
  1314.7 12.8 fusion.107
  1327.5 5.1 fusion.108
  1342.9 12.8 fusion.107
  1355.7 5.1 fusion.108
  1371.1 12.8 fusion.107
  1383.9 5.1 fusion.108
  1399.3 12.8 fusion.107
  1412.2 5.1 fusion.108
  1427.5 12.8 fusion.107
  1440.4 5.1 fusion.108
  1455.8 12.8 fusion.107
  1468.6 5.1 fusion.108
  1484.0 12.8 fusion.107
  1496.8 5.1 fusion.108
  1502.8 25.4 %convolution_bitcast_fusion = f32[8,8,128,2048]{3,2,0,1:T(8,128)} fusion(bf16[8,8,128,256]{2,3,1,0:T(8,128)(2,1)} %get-tuple-element.96, bf16[1,1280,2048]{2,1,0:T(8,128)(2,1)} %all-gather.31.cloned.1.call-done), kind=kOutput, calls=%fused_computation.70 | convolution fusion | flops 8589934592 | bytes 72351744 | tf_op jit(solution)/shard_map/nbqe,ed->bnqd/dot_general | solution.py:60
  1528.1 44.8 %copy.14 = f32[8,8,128,2048]{3,2,1,0:T(8,128)} copy(f32[8,8,128,2048]{3,2,0,1:T(8,128)} %convolution_bitcast_fusion) | data formatting | bytes 134217728 | tf_op jit(solution)/shard_map/nbqe,ed->bnqd/transpose | solution.py:60
  1572.9 53.5 %fusion.38 = bf16[8,1024,2048]{2,1,0:T(8,128)(2,1)} fusion(f32[8,8,128,2048]{3,2,1,0:T(8,128)} %copy.14, bf16[8,1024,2304]{2,1,0:T(8,128)(2,1)} %convolution_convert_fusion, bf16[1,1280,2048]{2,1,0:T(8,128)(2,1)} %all-gather.31.cloned.1.call-done), kind=kOutput, calls=%fused_computation.51 | convolution fusion | flops 34460401664 | bytes 138412032 | tf_op jit(solution)/shard_map/btf,fd->btd/dot_general | solution.py:61
  1626.4 168.2 %reduce-scatter.5.cloned.1.call-done = bf16[8,128,2048]{2,1,0:T(8,128)(2,1)} async-done(((bf16[8,1024,2048]{2,1,0:T(8,128)(2,1)}), bf16[8,128,2048]{2,1,0:T(8,128)(2,1)}) %reduce-scatter.5.cloned.1.call-update) | async-done | bytes 4194320 | tf_op jit(solution)/shard_map/reduce_scatter | solution.py:63
  1794.6 10.0 fusion.67
  (213 shorter events, 143.4 us)
Async XLA Ops:
  6.5 4.9 copy-start.8
  6.5 98.4 %all-gather.21.cloned.1.call-start = ((), (), s32[]{:S(2)}) async-start(), calls=%async_computation.6 | async-start | bytes 11796480 | tf_op jit(solution)/shard_map/all_gather | solution.py:47
  11.4 251.0 %all-gather.17.cloned.1.call-start = ((), (), s32[]{:S(2)}) async-start(), calls=%async_computation.2 | async-start | bytes 37748736 | tf_op jit(solution)/shard_map/all_gather | solution.py:51
  23.6 8.6 copy-start.5
  23.7 9.6 copy-start.2
  32.2 328.1 %all-gather.23.cloned.1.call-start = ((), (), s32[]{:S(2)}) async-start(), calls=%async_computation.7 | async-start | bytes 1310720 | tf_op jit(solution)/shard_map/all_gather | solution.py:48
  33.2 580.3 %all-gather.25.cloned.1.call-start = ((), (), s32[]{:S(2)}) async-start(), calls=%async_computation.8 | async-start | bytes 6553600 | tf_op jit(solution)/shard_map/all_gather | solution.py:49
  35.0 870.5 %reduce-scatter.3.cloned.1.call-start = ((), (), s32[]{:S(2)}) async-start(), calls=%async_computation.3 | async-start | bytes 37748736 | tf_op jit(solution)/shard_map/reduce_scatter | solution.py:63
  375.9 9.4 copy-start.6
  395.0 12.9 copy-start.4
  423.5 12.9 copy-start.4
  452.1 12.9 copy-start.4
  480.6 12.9 copy-start.4
  509.1 12.9 copy-start.4
  537.6 12.9 copy-start.4
  566.2 12.9 copy-start.4
  594.7 12.9 copy-start.4
  737.2 0.8 copy-start.9
  737.3 259.2 %all-gather.27.cloned.1.call-start = ((), (), s32[]{:S(2)}) async-start(), calls=%async_computation.9 | async-start | bytes 11796480 | tf_op jit(solution)/shard_map/all_gather | solution.py:47
  737.9 416.0 %all-gather.19.cloned.1.call-start = ((), (), s32[]{:S(2)}) async-start(), calls=%async_computation.4 | async-start | bytes 37748736 | tf_op jit(solution)/shard_map/all_gather | solution.py:51
  905.5 5.0 copy-start
  905.5 5.9 copy-start.1
  915.0 337.0 %all-gather.29.cloned.1.call-start = ((), (), s32[]{:S(2)}) async-start(), calls=%async_computation.10 | async-start | bytes 1310720 | tf_op jit(solution)/shard_map/all_gather | solution.py:48
  915.8 586.9 %all-gather.31.cloned.1.call-start = ((), (), s32[]{:S(2)}) async-start(), calls=%async_computation.11 | async-start | bytes 6553600 | tf_op jit(solution)/shard_map/all_gather | solution.py:49
  916.6 878.0 %reduce-scatter.5.cloned.1.call-start = ((), (), s32[]{:S(2)}) async-start(), calls=%async_computation.5 | async-start | bytes 37748736 | tf_op jit(solution)/shard_map/reduce_scatter | solution.py:63
  1267.7 9.3 copy-start.7
  1286.4 12.9 copy-start.3
  1314.6 12.9 copy-start.3
  1342.9 12.9 copy-start.3
  1371.1 12.9 copy-start.3
  1399.3 12.9 copy-start.3
  1427.5 12.9 copy-start.3
  1455.7 12.9 copy-start.3
  1484.0 12.9 copy-start.3
Sparse Core Ops, SparseCore 0:
  11.5 93.3 all-gather.20
  106.5 155.7 all-gather.16
  263.9 19.7 all-gather.22
  285.1 56.7 all-gather.24
  737.4 167.9 reduce-scatter.2
  906.9 89.5 all-gather.26
  998.1 155.7 all-gather.18
  1155.5 19.7 all-gather.28
  1176.8 56.7 all-gather.30
  1626.5 168.0 reduce-scatter.4
where the time goes:
time: 1820 us; the launch traced here: 1810 us
  waiting for transfers between devices  793 us (44%)
  matrix products  516 us (28%)
  other arithmetic  244 us (13%)
  local copies, waits for them, and re-layouts  185 us (10%)
  loops' own time  38.2 us (2%)
  blocking collectives  21.3 us (1%)
    reduce_scatter x2, waiting for transfers between devices, local_step(): z_sum = lax.psum_scatter(z_part, 'model', scatter_dimension=1, tiled=True)  326 us
    all_gather x2, waiting for transfers between devices, local_step(): h_full = lax.all_gather(normed, 'model', axis=1, tiled=True)  315 us
    sub x16, other arithmetic, one_block(): attn_probs = jax.nn.softmax(scores, axis=-1).astype(jnp.bfloat16)  205 us
    dot_general x2, matrix products, local_step(): jnp.einsum('btd,dc->btc', h_full, w_in_full, preferred_element_type=jnp.f...  173 us
    all_gather x2, waiting for transfers between devices, local_step(): w_in_full = lax.all_gather(w_in_loc[layer], 'data', axis=0, tiled=True)  149 us
    dot_general x2, matrix products, local_step(): jnp.einsum('btf,fd->btd', mlp_out, w_out_full[attn_cols:], preferred_elem...  107 us
    transpose x2, local copies, waits for them, and re-layouts, local_step(): jnp.einsum('nbqe,ed->bnqd', attn_blocks, w_out_full[:attn_cols], preferre...  89.5 us
    dot_general x16, matrix products, one_block(): jnp.einsum('cirl,cle->crie', attn_probs, values, preferred_element_type=j...  81.3 us
  transfers between devices with their start and end apart: 10, of which 6 were waited for; matrix products, arithmetic and copies ran while one was open for 38% of the time, Pallas kernels for 0%

commit v1 on v0

v1 whole, which is shorter than its diff:
```python
import functools

import jax
import jax.numpy as jnp
from jax import lax
from jax.experimental import pallas as pl
from jax.experimental.pallas import tpu as pltpu
from jax.sharding import PartitionSpec as P

EPSILON = 1e-6
VMEM_LIMIT = 66_000_000
MESH = pl.DeviceIdType.MESH
BF16, F32 = jnp.bfloat16, jnp.float32

UP, DOWN, FORWARD, FIRST, SIDE_UP, SIDE_DOWN, FAR, MATE, SIDE_MATE, KINDS = 0, 1, 2, 3, 4, 5, 6, 7, 11, 15


def rms_norm(x_in, gain):
    x_f32 = x_in.astype(F32)
    inv_rms = lax.rsqrt(jnp.mean(x_f32 * x_f32, axis=-1, keepdims=True) + EPSILON)
    return (x_f32 * inv_rms * gain.astype(F32)).astype(BF16)


class Place:
    def __init__(self, n_data, n_model, partner, neighbour):
        self.n_data, self.n_model = n_data, n_model
        self.y = lax.axis_index("data")
        self.me = lax.axis_index("model")
        self.up = lax.rem(self.y + 1, n_data)
        self.down = lax.rem(self.y + n_data - 1, n_data)
        self.far = lax.rem(self.y + 2, n_data)
        self.slots = (self.y, self.down, self.up, self.far)
        self.mate = self.me + 1 - 2 * lax.rem(self.me, 2)
        self.partner, self.neighbour = partner(self.me), neighbour(self.me)
        n_other = n_model // 2 - 1
        self.ahead = [lax.rem(self.me + 2 * k, n_model) for k in range(1, n_other + 1)]
        self.behind = [lax.rem(self.me + n_model - 2 * k, n_model) for k in range(1, n_other + 1)]

    def meet(self):
        barrier = pltpu.get_barrier_semaphore()
        targets = [{"data": self.up}, {"data": self.down}, {"data": self.far}, {"model": self.mate}]
        targets += [{"model": m} for m in self.ahead]
        for target in targets:
            pl.semaphore_signal(barrier, inc=1, device_id=target, device_id_type=MESH)
        pl.semaphore_wait(barrier, len(targets))


def remote(src, dst, send, recv, target):
    return pltpu.make_async_remote_copy(
        src_ref=src, dst_ref=dst, send_sem=send, recv_sem=recv, device_id=target, device_id_type=MESH
    )


class Gather:
    def __init__(self, place, buf, own, send, recv, local, first=None, column=None):
        self.place, self.buf, self.own, self.first, self.column = place, buf, own, first, column
        self.send, self.recv, self.local = send, recv, local

    def at(self, block, p, slot):
        return self.buf.at[block, p, slot]

    def _copy(self, src, dst, kind, p, target):
        return remote(src, dst, self.send.at[kind, p], self.recv.at[kind, p], target)

    def up(self, p):
        y = self.place.y
        return self._copy(self.own(p), self.at(0, p, y), UP, p, {"data": self.place.up})

    def down(self, p):
        y = self.place.y
        return self._copy(self.own(p), self.at(0, p, y), DOWN, p, {"data": self.place.down})

    def forward(self, p):
        even = lax.rem(p, 2) == 0
        slot = jnp.where(even, self.place.down, self.place.up)
        target = jnp.where(even, self.place.up, self.place.down)
        return self._copy(self.at(0, p, slot), self.at(0, p, slot), FORWARD, p, {"data": target})

    def neighbour_first(self, p):
        return self._copy(self.own(p), self.at(2, p, self.place.y), FIRST, p, {"model": self.place.neighbour})

    def _first(self, p):
        return self.at(2, p, self.place.y) if self.first is None else self.first.at[p]

    def side_up(self, p):
        return self._copy(self._first(p), self.at(2, p, self.place.y), SIDE_UP, p, {"data": self.place.up})

    def side_down(self, p):
        return self._copy(self._first(p), self.at(2, p, self.place.y), SIDE_DOWN, p, {"data": self.place.down})

    def neighbour_far(self, p):
        far = self.place.far
        src = self.at(0, p, far) if self.column is None else self.column.at[p, far]
        return self._copy(src, self.at(2, p, far), FAR, p, {"model": self.place.neighbour})

    def mate(self, p, which):
        slot = self.place.slots[which]
        if which == 0:
            src = self.own(p)
        else:
            src = self.at(0, p, slot) if self.column is None else self.column.at[p, slot]
        return self._copy(src, self.at(1, p, slot), MATE + which, p, {"model": self.place.mate})

    def side_mate(self, p, which):
        slot = self.place.slots[which]
        src = self._first(p) if which == 0 else self.at(2, p, slot)
        return self._copy(src, self.at(3, p, slot), SIDE_MATE + which, p, {"model": self.place.mate})

    def load_own(self, p):
        return pltpu.make_async_copy(self.own(p), self.at(0, p, self.place.y), self.local.at[0, p])

    def load_column(self, p, which):
        slot = self.place.slots[which]
        return pltpu.make_async_copy(self.column.at[p, slot], self.at(0, p, slot), self.local.at[which, p])

    def load_first(self, p):
        return pltpu.make_async_copy(self.first.at[p], self.at(2, p, self.place.y), self.local.at[4, p])

    def pass_side(self, p):
        self.side_up(p).wait_recv()
        self.side_mate(p, 1).start()
        self.side_down(p).wait_recv()
        self.side_mate(p, 2).start()
        self.neighbour_far(p).wait_recv()
        self.side_mate(p, 3).start()

    def wait_sends(self, p):
        made = [self.side_up(p), self.side_down(p), self.neighbour_far(p)]
        if self.column is None:
            made += [self.up(p), self.down(p), self.forward(p)]
        if self.first is None:
            made.append(self.neighbour_first(p))
        made += [self.mate(p, which) for which in range(4)] + [self.side_mate(p, which) for which in range(4)]
        for copy in made:
            copy.wait_send()


class Prefetch:
    def __init__(self, place, own, send, recv, neighbour=None, first=None, column=None):
        self.place, self.own, self.send, self.recv = place, own, send, recv
        self.neighbour, self.first, self.column = neighbour, first, column

    def up(self, p):
        dst = self.column.at[p, self.place.y]
        return remote(self.own(p), dst, self.send.at[0, p], self.recv.at[0, p], {"data": self.place.up})

    def down(self, p):
        dst = self.column.at[p, self.place.y]
        return remote(self.own(p), dst, self.send.at[1, p], self.recv.at[1, p], {"data": self.place.down})

    def forward(self, p):
        even = lax.rem(p, 2) == 0
        slot = jnp.where(even, self.place.down, self.place.up)
        target = jnp.where(even, self.place.up, self.place.down)
        ref = self.column.at[p, slot]
        return remote(ref, ref, self.send.at[2, p], self.recv.at[2, p], {"data": target})

    def neighbour_first(self, p):
        return remote(self.own(p), self.first.at[p], self.send.at[3, p], self.recv.at[3, p], {"model": self.neighbour})


def in_pieces(layer, head_ref, w_ref, c, ff):
    def own(p):
        if isinstance(p, int) and p < 2:
            return head_ref.at[layer, :, pl.ds(p * c, c)]
        column = (p // 2) * c + lax.rem(p, 2) * ff
        return w_ref.at[layer, :, pl.ds(pl.multiple_of(column, c), c)]

    return own


def out_pieces(layer, w_ref, width):
    def own(p):
        return w_ref.at[layer, :, pl.ds(pl.multiple_of(p * width, width), width)]

    return own


def project(layer, n_data, n_model, partner, neighbour, next_neighbour, x_own, head, w_in, w_out, extra):
    start_layer = layer == 0
    rows, d_model = x_own.shape
    part, two_c = head.shape[1:]
    c = two_c // 2
    depth, out_part = w_out.shape[1:]
    ff = depth - c
    n_group = 1 + ff // c
    pieces = 2 * n_group
    width = out_part // 2
    n_units = 8 * n_group
    row_parts = 4
    row_part = rows // row_parts
    n_other = n_model // 2 - 1
    gain_shape = (n_data, 8, part)

    def kernel(*refs):
        x_ref, head_ref, w_ref, wo_ref = refs[:4]
        if start_layer:
            gain_ref = refs[4]
            q_ref, m_ref, kv_ref, gains_ref, out_first_ref, in_first_ref = refs[5:11]
            first_ref = column_ref = None
            rest = refs[11:]
        else:
            par_ref, gain_ref, first_ref, column_ref = refs[4:8]
            q_ref, m_ref, kv_ref, out_first_ref, out_column_ref = refs[8:13]
            rest = refs[13:]
        wbuf, h_ref, gbuf, stage, kv_stage, send, recv, w_local, next_send, next_recv, late_send, late_recv = rest[:12]
        x_send, x_recv, g_send, g_recv, kv_send, kv_recv, local, out_sem = rest[12:]

        place = Place(n_data, n_model, partner, neighbour)
        place.meet()
        w = Gather(place, wbuf, in_pieces(layer, head_ref, w_ref, c, ff), send, recv, w_local, first_ref, column_ref)
        out_own = out_pieces(layer, wo_ref, width)
        if start_layer:
            out_next = Prefetch(place, out_own, next_send, next_recv, place.neighbour, out_first_ref)
            in_own = in_pieces(layer + 1, head_ref, w_ref, c, ff)
            in_next = Prefetch(place, in_own, late_send, late_recv, next_neighbour(place.me), in_first_ref)
        else:
            out_next = Prefetch(place, out_own, next_send, next_recv, place.neighbour, out_first_ref, out_column_ref)

        def c_x(part_no):
            piece = pl.ds(part_no * row_part, row_part)
            return remote(
                x_ref.at[piece], h_ref.at[1, piece], x_send.at[part_no], x_recv.at[part_no], {"model": place.partner}
            )

        def c_gain(which):
            target = {"data": (place.up, place.down, place.far)[which]}
            return remote(gain_ref, gbuf.at[place.y], g_send.at[which], g_recv.at[which], target)

        def c_kv(which):
            ref = kv_ref.at[place.me]
            return remote(ref, ref, kv_send.at[which], kv_recv.at[which], {"model": place.ahead[which]})

        def c_kv_mate(which):
            ref = kv_ref.at[place.me if which == 0 else place.behind[which - 1]]
            at = n_other + which
            return remote(ref, ref, kv_send.at[at], kv_recv.at[at], {"model": place.mate})

        save_kv = pltpu.make_async_copy(kv_stage, kv_ref.at[place.me], local.at[0])
        load_x = pltpu.make_async_copy(x_ref, h_ref.at[0], local.at[0])

        if start_layer:
            load_gain = pltpu.make_async_copy(gain_ref, gbuf.at[place.y], local.at[1])
            for which in range(3):
                c_gain(which).start()
        else:
            load_gain = pltpu.make_async_copy(gain_ref, gbuf, local.at[1])
            load_par = pltpu.make_async_copy(par_ref, h_ref.at[1], local.at[2])
        load_gain.start()
        load_x.start()
        if start_layer:
            for p in range(4):
                w.up(p).start()
                w.down(p).start()
            for p in range(pieces):
                w.neighbour_first(p).start()
                w.load_own(p).start()
            for part_no in range(row_parts):
                c_x(part_no).start()
            for p in range(pieces):
                w.mate(p, 0).start()
        else:
            load_par.start()
            for p in range(pieces):
                w.load_own(p).start()
                for which in range(1, 4):
                    w.load_column(p, which).start()
                w.mate(p, 0).start()
                w.side_up(p).start()
                w.side_down(p).start()
                w.neighbour_far(p).start()
                for which in range(1, 4):
                    w.mate(p, which).start()
            for p in range(pieces):
                w.load_first(p).start()
                w.side_mate(p, 0).start()
            for p in range(2):
                out_next.neighbour_first(p).start()
                out_next.up(p).start()
                out_next.down(p).start()

        def ring_stage(g):
            for p in (2 * g, 2 * g + 1):
                w.up(p).wait_recv()
                w.down(p).wait_recv()
                w.forward(p).start()

            @pl.when(g + 2 < n_group)
            def _():
                for p in (2 * g + 4, 2 * g + 5):
                    w.up(p).start()
                    w.down(p).start()

            for p in (2 * g, 2 * g + 1):
                w.mate(p, 1).start()
                w.mate(p, 2).start()

        if start_layer:
            for which in range(3):
                c_gain(which).wait_recv()
        load_gain.wait()
        gain = jnp.concatenate([gbuf[k, layer:layer + 1, :] for k in range(n_data)], axis=1)
        if start_layer:
            save_gain = pltpu.make_async_copy(gbuf, gains_ref, local.at[1])
            save_gain.start()
        load_x.wait()

        def norm_rows(side, part_no):
            piece = pl.ds(part_no * row_part, row_part)
            h_ref[side, piece] = rms_norm(h_ref[side, piece], gain)

        @pl.loop(0, row_parts)
        def _(part_no):
            norm_rows(0, part_no)

        if start_layer:
            ring_stage(0)
        else:
            load_par.wait()

            @pl.loop(0, row_parts)
            def _(part_no):
                norm_rows(1, part_no)

        half, quarter = n_units // 2, n_units // 4

        def out_copy(slot, blk, side, g):
            def to_q():
                return pltpu.make_async_copy(stage.at[slot], q_ref.at[blk, side], out_sem.at[slot])

            def to_m():
                column = pl.ds(pl.multiple_of((g - 1) * c, c), c)
                return pltpu.make_async_copy(stage.at[slot], m_ref.at[blk, side, :, column], out_sem.at[slot])

            return to_q, to_m

        @pl.loop(0, n_units)
        def _(step):
            late = step - half
            if start_layer:
                opening, second = step < quarter, (step >= quarter) & (step < half)
                g = jnp.where(opening, step // 2, jnp.where(second, (step - quarter) // 2, late // 4))
                blk = jnp.where(step < half, lax.rem(step, 2), 2 + lax.rem(late, 4) // 2)
                side = jnp.where(opening, 0, jnp.where(second, 1, lax.rem(late, 2)))

                @pl.when(opening & (blk == 0))
                def _():
                    @pl.when(g + 1 < n_group)
                    def _():
                        ring_stage(g + 1)

                    @pl.when(g + 2 == n_group)
                    def _():
                        @pl.loop(0, pieces)
                        def _(p):
                            w.neighbour_first(p).wait_recv()
                            w.side_up(p).start()
                            w.side_down(p).start()
                            w.side_mate(p, 0).start()

                    for p in (2 * g, 2 * g + 1):
                        w.forward(p).wait_recv()
                        w.mate(p, 3).start()
                        w.neighbour_far(p).start()
                        w.load_own(p).wait()

                @pl.when(opening & (blk == 1))
                def _():
                    for p in (2 * g, 2 * g + 1):
                        for which in range(4):
                            w.mate(p, which).wait_recv()

                @pl.when(step == quarter)
                def _():
                    @pl.loop(0, row_parts)
                    def _(part_no):
                        c_x(part_no).wait_recv()
                        norm_rows(1, part_no)

                    for p in range(2):
                        out_next.neighbour_first(p).start()
                    for p in range(pieces):
                        in_next.neighbour_first(p).start()
            else:
                g = jnp.where(late < 0, step, late) // 4
                blk = jnp.where(late < 0, 0, 2) + lax.rem(step, 4) // 2
                side = lax.rem(step, 2)

                @pl.when((late < 0) & (lax.rem(step, 4) == 0))
                def _():
                    for p in (2 * g, 2 * g + 1):
                        w.load_own(p).wait()
                        for which in range(1, 4):
                            w.load_column(p, which).wait()

                @pl.when((late < 0) & (lax.rem(step, 4) == 2))
                def _():
                    for p in (2 * g, 2 * g + 1):
                        for which in range(4):
                            w.mate(p, which).wait_recv()

                @pl.when(step == half - 2)
                def _():
                    @pl.loop(0, pieces)
                    def _(p):
                        w.load_first(p).wait()

                @pl.when(step == n_units - 4)
                def _():
                    for p in range(2):
                        out_next.up(p).wait_recv()
                        out_next.down(p).wait_recv()
                        out_next.forward(p).start()

            @pl.when(step == half - 2)
            def _():
                for p in range(2):
                    w.pass_side(p)

            @pl.when((late >= 0) & (lax.rem(late, 4) == 2))
            def _():
                @pl.when(g + 1 < n_group)
                def _():
                    for p in (2 * g + 2, 2 * g + 3):
                        w.pass_side(p)

                for p in (2 * g, 2 * g + 1):
                    for which in range(4):
                        w.side_mate(p, which).wait_recv()

            slot = lax.rem(step, 2)
            to_q, to_m = out_copy(slot, blk, side, g)

            @pl.when(step >= 2)
            def _():
                to_q().wait()

            def columns(p):
                return wbuf[blk, p].reshape(d_model, c)

            @pl.when(g == 0)
            def _():
                q = jnp.dot(h_ref[side], columns(0), preferred_element_type=F32)
                stage[slot] = q.astype(BF16)
                to_q().start()

            @pl.when(g > 0)
            def _():
                h_val = h_ref[side]
                gate = jnp.dot(h_val, columns(2 * g), preferred_element_type=F32).astype(BF16).astype(F32)
                raised = jnp.dot(h_val, columns(2 * g + 1), preferred_element_type=F32).astype(BF16).astype(F32)
                stage[slot] = (gate * jax.nn.sigmoid(gate) * raised).astype(BF16)
                to_m().start()

            @pl.when(step == 0)
            def _():
                kv_stage[...] = jnp.dot(h_ref[0], columns(1), preferred_element_type=F32).astype(BF16)
                save_kv.start()

            @pl.when(step == 1)
            def _():
                save_kv.wait()
                for which in range(n_other):
                    c_kv(which).start()
                c_kv_mate(0).start()

            @pl.when(step == quarter)
            def _():
                for which in range(n_other):
                    c_kv(which).wait_recv()
                    c_kv_mate(1 + which).start()

        for which in range(n_other + 1):
            c_kv_mate(which).wait()
        for which in range(n_other):
            c_kv(which).wait_send()
        if start_layer:
            save_gain.wait()
            for which in range(3):
                c_gain(which).wait_send()
            for part_no in range(row_parts):
                c_x(part_no).wait_send()
            for p in range(pieces):
                in_next.neighbour_first(p).wait()
        else:
            for p in range(2):
                out_next.forward(p).wait()
                out_next.up(p).wait_send()
                out_next.down(p).wait_send()
        for p in range(2):
            out_next.neighbour_first(p).wait()
        for slot in range(2):
            pltpu.make_async_copy(stage.at[slot], q_ref.at[0, 0], out_sem.at[slot]).wait()

        @pl.loop(0, pieces)
        def _(p):
            w.wait_sends(p)

    anywhere = pl.BlockSpec(memory_space=pl.ANY)
    out_shape = [
        jax.ShapeDtypeStruct((4, 2, rows, c), BF16),
        jax.ShapeDtypeStruct((4, 2, rows, ff), BF16),
        jax.ShapeDtypeStruct((n_model, rows, c), BF16),
    ]
    if start_layer:
        out_shape += [
            jax.ShapeDtypeStruct(gain_shape, F32),
            jax.ShapeDtypeStruct((2, depth, width), BF16),
            jax.ShapeDtypeStruct((pieces, part, c), BF16),
        ]
    else:
        out_shape += [
            jax.ShapeDtypeStruct((2, depth, width), BF16),
            jax.ShapeDtypeStruct((2, n_data, depth, width), BF16),
        ]
    dma = pltpu.SemaphoreType.DMA
    args = (x_own, head, w_in, w_out) + tuple(extra)
    return pl.pallas_call(
        kernel,
        out_shape=out_shape,
        in_specs=[anywhere] * len(args),
        out_specs=[anywhere] * len(out_shape),
        scratch_shapes=[
            pltpu.VMEM((4, pieces, n_data, part, c), BF16),
            pltpu.VMEM((2, rows, d_model), BF16),
            pltpu.VMEM(gain_shape, F32),
            pltpu.VMEM((2, rows, c), BF16),
            pltpu.VMEM((rows, c), BF16),
            dma((KINDS, pieces)), dma((KINDS, pieces)), dma((5, pieces)),
            dma((4, 2)), dma((4, 2)), dma((4, pieces)), dma((4, pieces)),
            dma((row_parts,)), dma((row_parts,)), dma((3,)), dma((3,)),
            dma((n_model - 1,)), dma((n_model - 1,)), dma((3,)), dma((2,)),
        ],
        compiler_params=pltpu.CompilerParams(collective_id=2 * layer, has_side_effects=True, vmem_limit_bytes=VMEM_LIMIT),
        cost_estimate=pl.CostEstimate(flops=4 * rows * d_model * 4 * (c + 2 * ff), bytes_accessed=16 * rows * d_model, transcendentals=0),
        name=f"project_{layer}",
    )(*args)


def attend_and_sum(layer, last, n_data, n_model, partner, neighbour, next_partner, lens, q, m, kv, x_own, w_in, w_out, head, first, column):
    n_blocks, _, rows, c = q.shape
    ff = m.shape[3]
    d_model = x_own.shape[1]
    depth, out_part = w_out.shape[1:]
    width = out_part // 2
    head_dim = c // 2
    n_batch = lens.shape[0]
    slab_len = rows // n_batch
    chunks = 4
    n_seq = n_batch // chunks
    crow = rows // chunks
    tiles = chunks * n_data
    heads = n_blocks * 2
    qrows = heads * slab_len
    key_rows = 2 * slab_len
    scale = head_dim ** -0.5 * 1.4426950408889634
    part = head.shape[1]
    in_count = 2 * (1 + ff // c)
    ready = column is not None
    held = tiles // 2

    def kernel(*refs):
        lens_ref, q_ref, m_ref, kv_ref, x_ref, wo_ref, first_ref = refs[:7]
        at = 7
        column_ref = None
        if ready:
            column_ref = refs[at]
            at += 1
        if not last:
            head_ref, wi_ref = refs[at:at + 2]
            at += 2
        y_ref = refs[at]
        at += 1
        if not last:
            par_ref, in_column_ref = refs[at:at + 2]
            at += 2
        (wbuf, obuf, kvb, mbuf, xb, zb, zr, z_stage, s_ref, mx_ref, sum_ref, acc_ref,
         send, recv, w_local, in_send, in_recv, z_send, z_recv, y_send, y_recv, y_save, x_sem, m_sem, local) = refs[at:]

        place = Place(n_data, n_model, partner, neighbour)
        place.meet()
        w = Gather(place, wbuf, out_pieces(layer, wo_ref, width), send, recv, w_local, first_ref, column_ref)

        def tile_of(k):
            which = k // chunks
            slot = jnp.where(which == 0, place.y, jnp.where(which == 1, place.down, jnp.where(which == 2, place.up, place.far)))
            return lax.rem(k, chunks), which, slot

        def whole(ref, chunk, slot):
            return ref.at[pl.ds(pl.multiple_of(chunk * crow, crow), crow), pl.ds(pl.multiple_of(slot * out_part, out_part), out_part)]

        load_q = pltpu.make_async_copy(q_ref, obuf, local.at[0])
        load_kv = pltpu.make_async_copy(kv_ref, kvb, local.at[1])

        def load_m(k):
            chunk, _, _ = tile_of(k)
            slot = lax.rem(k, 2)
            return pltpu.make_async_copy(
                m_ref.at[:, :, pl.ds(pl.multiple_of(chunk * crow, crow), crow)], mbuf.at[slot], m_sem.at[slot]
            )

        def load_x(k):
            chunk, _, slot = tile_of(k)
            return pltpu.make_async_copy(whole(x_ref, chunk, slot), xb.at[chunk, slot], x_sem.at[k])

        def c_z(k):
            chunk, _, slot = tile_of(k)
            return remote(z_stage.at[lax.rem(k, 4)], zr.at[chunk, slot], z_send.at[k], z_recv.at[k], {"model": place.partner})

        def c_y(k):
            chunk, _, slot = tile_of(k)
            target = {"model": next_partner(place.me)}
            return remote(xb.at[chunk, slot], whole(par_ref, chunk, slot), y_send.at[k], y_recv.at[k], target)

        def save_y(k):
            chunk, _, slot = tile_of(k)
            return pltpu.make_async_copy(xb.at[chunk, slot], whole(y_ref, chunk, slot), y_save.at[k])

        load_q.start()
        load_kv.start()
        load_m(0).start()
        for p in range(2):
            w.load_own(p).start()
            w.load_first(p).start()
            w.mate(p, 0).start()
            w.side_mate(p, 0).start()
        for p in range(2):
            if ready:
                for which in range(1, 4):
                    w.load_column(p, which).start()
                    w.mate(p, which).start()
                w.neighbour_far(p).start()
            else:
                w.up(p).start()
                w.down(p).start()
        for p in range(2):
            w.side_up(p).start()
            w.side_down(p).start()
        if not last:
            in_next = Prefetch(place, in_pieces(layer + 1, head_ref, wi_ref, c, ff), in_send, in_recv, column=in_column_ref)

        @pl.loop(0, tiles)
        def _(k):
            load_x(k).start()

        load_q.wait()
        load_kv.wait()

        def attend_one(batch, side):
            slab = jnp.where(side == 0, place.me, place.partner)
            length = lens_ref[batch]
            n_key = slab // 2 + 1
            at_row = pl.ds(pl.multiple_of(batch * slab_len, slab_len), slab_len)
            parts = []
            for blk in range(n_blocks):
                for one in range(2):
                    parts.append(obuf[blk, side, at_row, one * head_dim:(one + 1) * head_dim])
            q_val = jnp.concatenate(parts, axis=0)
            row_pos = slab * slab_len + lax.rem(lax.broadcasted_iota(jnp.int32, (qrows, key_rows), 0), slab_len)
            key_pos = lax.broadcasted_iota(jnp.int32, (qrows, key_rows), 1)
            room = jnp.minimum(row_pos + 1, length) - key_pos
            mx_ref[...] = jnp.full_like(mx_ref, -1e30)

            def score(kb, carry):
                k = kvb[pl.ds(2 * kb, 2), at_row, :head_dim].reshape(key_rows, head_dim)
                s = lax.dot_general(q_val, k, (((1,), (1,)), ((), ())), preferred_element_type=F32) * scale
                s = jnp.where(room > kb * key_rows, s, -1e30)
                s_ref[kb] = s
                mx_ref[...] = jnp.maximum(mx_ref[...], jnp.maximum(s[:, :slab_len], s[:, slab_len:]))
                return carry

            lax.fori_loop(0, n_key, score, 0)
            top = jnp.max(mx_ref[...], axis=-1, keepdims=True)
            mx_ref[...] = jnp.broadcast_to(top, mx_ref.shape)
            sum_ref[...] = jnp.zeros_like(sum_ref)
            acc_ref[...] = jnp.zeros_like(acc_ref)

            def weigh(kb, carry):
                v = kvb[pl.ds(2 * kb, 2), at_row, head_dim:].reshape(key_rows, head_dim)
                top_b = mx_ref[...]
                e_lo = jnp.exp2(s_ref[kb, :, :slab_len] - top_b)
                e_hi = jnp.exp2(s_ref[kb, :, slab_len:] - top_b)
                sum_ref[...] += e_lo + e_hi
                e = jnp.concatenate([e_lo, e_hi], axis=1).astype(BF16)
                acc_ref[...] += jnp.dot(e, v, preferred_element_type=F32)
                return carry

            lax.fori_loop(0, n_key, weigh, 0)
            out = (acc_ref[...] / jnp.sum(sum_ref[...], axis=-1, keepdims=True)).astype(BF16)
            for blk in range(n_blocks):
                for one in range(2):
                    first_row = (blk * 2 + one) * slab_len
                    obuf[blk, side, at_row, one * head_dim:(one + 1) * head_dim] = out[first_row:first_row + slab_len]

        def settle(k):
            chunk, _, slot = tile_of(k)
            load_x(k).wait()
            c_z(k).wait_recv()
            z = zb[chunk, slot].astype(F32) + zr[chunk, slot].astype(F32)
            xb[chunk, slot] = (xb[chunk, slot].astype(F32) + z).astype(BF16)
            save_y(k).start()
            if not last:
                c_y(k).start()

        @pl.loop(0, tiles)
        def _(step):
            chunk, which, slot = tile_of(step)

            @pl.when(step + 1 < tiles)
            def _():
                load_m(step + 1).start()

            @pl.when(step < chunks)
            def _():
                @pl.loop(0, 2 * n_seq)
                def _(unit):
                    attend_one(step * n_seq + unit // 2, lax.rem(unit, 2))

            @pl.when(step == 0)
            def _():
                for p in range(2):
                    w.load_own(p).wait()
                    w.load_first(p).wait()
                    w.mate(p, 0).wait_recv()
                    w.side_mate(p, 0).wait_recv()

            if not ready:

                @pl.when(step == 2)
                def _():
                    for p in range(2):
                        w.up(p).wait_recv()
                        w.down(p).wait_recv()
                        w.forward(p).start()
                        w.mate(p, 1).start()
                        w.mate(p, 2).start()
                    if not last:
                        for p in range(4):
                            in_next.up(p).start()
                            in_next.down(p).start()

                @pl.when(step == chunks + 2)
                def _():
                    for p in range(2):
                        w.forward(p).wait_recv()
                        w.mate(p, 3).start()
                        w.neighbour_far(p).start()

            @pl.when(step == chunks)
            def _():
                for p in range(2):
                    w.side_up(p).wait_recv()
                    w.side_mate(p, 1).start()
                    w.side_down(p).wait_recv()
                    w.side_mate(p, 2).start()
                for p in range(2):
                    for one in (1, 2):
                        if ready:
                            w.load_column(p, one).wait()
                        w.mate(p, one).wait_recv()
                        w.side_mate(p, one).wait_recv()

            @pl.when(step == 3 * chunks)
            def _():
                for p in range(2):
                    w.neighbour_far(p).wait_recv()
                    w.side_mate(p, 3).start()
                for p in range(2):
                    if ready:
                        w.load_column(p, 3).wait()
                    w.mate(p, 3).wait_recv()
                    w.side_mate(p, 3).wait_recv()

            if not last:
                @pl.when((step >= chunks + 3) & (lax.rem(step, 2) == 1))
                def _():
                    g = (step - chunks - 3) // 2

                    @pl.when(g < in_count // 2 - 2)
                    def _():
                        for p in (2 * g + 4, 2 * g + 5):
                            in_next.up(p).start()
                            in_next.down(p).start()

            @pl.when(step >= 4)
            def _():
                c_z(step - 4).wait_send()

            load_m(step).wait()
            here = lax.rem(step, 2)
            rows_c = pl.ds(pl.multiple_of(chunk * crow, crow), crow)
            for p in range(2):
                total = None
                for blk in range(n_blocks):
                    mid = mbuf[here, blk].reshape(2 * crow, ff)
                    attn = obuf[blk, :, rows_c, :].reshape(2 * crow, c)
                    one = jnp.dot(mid, wbuf[blk, p, slot, c:, :], preferred_element_type=F32)
                    one = one + jnp.dot(attn, wbuf[blk, p, slot, :c, :], preferred_element_type=F32)
                    total = one if total is None else total + one
                z = total.astype(BF16)
                zb[chunk, slot, :, p * width:(p + 1) * width] = z[:crow]
                z_stage[lax.rem(step, 4), :, p * width:(p + 1) * width] = z[crow:]
            c_z(step).start()

            early = (step >= 1) & (step <= chunks)
            paced = (step >= 2 * chunks) & (lax.rem(step, 2) == 0)

            @pl.when(early | paced)
            def _():
                settle(jnp.where(early, step - 1, step // 2))

        if not last:

            @pl.loop(0, in_count)
            def _(p):
                in_next.up(p).wait_recv()
                in_next.down(p).wait_recv()
                in_next.forward(p).start()

        @pl.loop(held, tiles)
        def _(k):
            settle(k)

        @pl.loop(0, tiles)
        def _(k):
            save_y(k).wait()
            if not last:
                c_y(k).wait()

        @pl.loop(tiles - 4, tiles)
        def _(k):
            c_z(k).wait_send()

        for p in range(2):
            w.wait_sends(p)
        if not last:

            @pl.loop(0, in_count)
            def _(p):
                in_next.forward(p).wait()
                in_next.up(p).wait_send()
                in_next.down(p).wait_send()

    anywhere = pl.BlockSpec(memory_space=pl.ANY)
    args = [lens, q, m, kv, x_own, w_out, first]
    if ready:
        args.append(column)
    if not last:
        args += [head, w_in]
    out_shape = [jax.ShapeDtypeStruct((rows, d_model), BF16)]
    if not last:
        out_shape += [
            jax.ShapeDtypeStruct((rows, d_model), BF16),
            jax.ShapeDtypeStruct((in_count, n_data, part, c), BF16),
        ]
    dma = pltpu.SemaphoreType.DMA
    tile = (chunks, n_data, crow, out_part)
    return pl.pallas_call(
        kernel,
        out_shape=out_shape,
        in_specs=[pl.BlockSpec(memory_space=pltpu.SMEM)] + [anywhere] * (len(args) - 1),
        out_specs=[anywhere] * len(out_shape),
        scratch_shapes=[
            pltpu.VMEM((n_blocks, 2, n_data, depth, width), BF16),
            pltpu.VMEM(q.shape, BF16),
            pltpu.VMEM(kv.shape, BF16),
            pltpu.VMEM((2, n_blocks, 2, crow, ff), BF16),
            pltpu.VMEM(tile, BF16),
            pltpu.VMEM(tile, BF16),
            pltpu.VMEM(tile, BF16),
            pltpu.VMEM((4, crow, out_part), BF16),
            pltpu.VMEM((n_model // 2, qrows, key_rows), F32),
            pltpu.VMEM((qrows, slab_len), F32),
            pltpu.VMEM((qrows, slab_len), F32),
            pltpu.VMEM((qrows, head_dim), F32),
            dma((KINDS, 2)), dma((KINDS, 2)), dma((5, 2)), dma((4, in_count)), dma((4, in_count)),
            dma((tiles,)), dma((tiles,)), dma((tiles,)), dma((tiles,)), dma((tiles,)), dma((tiles,)), dma((2,)), dma((2,)),
        ],
        compiler_params=pltpu.CompilerParams(collective_id=2 * layer + 1, has_side_effects=True, vmem_limit_bytes=VMEM_LIMIT),
        cost_estimate=pl.CostEstimate(flops=4 * rows * n_blocks * depth * d_model, bytes_accessed=16 * rows * d_model, transcendentals=0),
        name=f"attend_and_sum_{layer}",
    )(*args)


def solution(mesh):
    batch_axes = ("rep", "data")
    n_data, n_model = mesh.shape["data"], mesh.shape["model"]
    n_chip = n_model // 2

    def near(x):
        return x + 1 - 2 * (x % 2)

    def across(x):
        return n_chip - 1 - x

    def on_chip(other):
        return lambda m: 2 * other(m // 2) + m % 2

    def local_step(x_loc, lens_loc, gamma_loc, w_in_loc, w_kv_loc, w_out_loc):
        n_batch, slab_len, d_model = x_loc.shape
        n_layers, part = gamma_loc.shape
        attn_cols = w_kv_loc.shape[2]
        partners = [on_chip(near if layer % 2 == 0 else across) for layer in range(n_layers)]
        neighbours = [on_chip(across if layer % 2 == 0 else near) for layer in range(n_layers)]

        head = jnp.concatenate([w_in_loc[:, :, :attn_cols], w_kv_loc], axis=2)
        gain_rows = jnp.zeros((8, part), F32).at[:n_layers].set(gamma_loc.astype(F32))
        own = x_loc.reshape(n_batch * slab_len, d_model)
        for layer in range(n_layers):
            last = layer + 1 == n_layers
            following = min(layer + 1, n_layers - 1)
            if layer == 0:
                extra = (gain_rows,)
                q, m, kv, gains, out_first, in_first = project(
                    layer, n_data, n_model, partners[layer], neighbours[layer], neighbours[following],
                    own, head, w_in_loc, w_out_loc, extra,
                )
                out_column = None
            else:
                extra = (other, gains, in_first, in_column)
                q, m, kv, out_first, out_column = project(
                    layer, n_data, n_model, partners[layer], neighbours[layer], neighbours[following],
                    own, head, w_in_loc, w_out_loc, extra,
                )
            outs = attend_and_sum(
                layer, last, n_data, n_model, partners[layer], neighbours[layer], partners[following],
                lens_loc, q, m, kv, own, w_in_loc, w_out_loc, head, out_first, out_column,
            )
            own = outs[0]
            if not last:
                other, in_column = outs[1:]
        return own.reshape(n_batch, slab_len, d_model)

    in_specs = (
        P(batch_axes, "model", None),
        P(batch_axes),
        P(None, "data"),
        P(None, "data", "model"),
        P(None, "data", None),
        P(None, "model", "data"),
    )
    return jax.shard_map(local_step, mesh=mesh, in_specs=in_specs, out_specs=P(batch_axes, "model", None), check_vma=False)
```

time: 1820 us -> 702 us (0.39)
  waiting for transfers between devices: 793 us -> 0 us
  Pallas kernels: 0 us -> 693 us
  matrix products: 516 us -> 0 us
  other arithmetic: 244 us -> 3.37 us
  local copies, waits for them, and re-layouts: 185 us -> 5.86 us
  loops' own time: 38.2 us -> 0 us
  blocking collectives: 21.3 us -> 0 us
    pallas_call x0 -> x4, Pallas kernels: none -> 693 us  [the longest x2 379 us: project(): pl.pallas_call(kernel, out_shape=out_shape, in_specs=[anywhere] * len(arg...]
    dot_general x40 -> x0, matrix products: 516 us -> none  [the longest x2 173 us: local_step(): jnp.einsum('btd,dc->btc', h_full, w_in_full, preferred_element_type=jnp.f...]
    all_gather x8 -> x0, waiting for transfers between devices: 464 us -> none  [the longest x2 315 us: local_step(): h_full = lax.all_gather(normed, 'model', axis=1, tiled=True)]
    reduce_scatter x2 -> x0, waiting for transfers between devices: 326 us -> none  [local_step(): z_sum = lax.psum_scatter(z_part, 'model', scatter_dimension=1, tiled=True)]
    sub x16 -> x0, other arithmetic: 205 us -> none  [one_block(): attn_probs = jax.nn.softmax(scores, axis=-1).astype(jnp.bfloat16)]
    transpose x2 -> x0, local copies, waits for them, and re-layouts: 89.5 us -> none  [local_step(): jnp.einsum('nbqe,ed->bnqd', attn_blocks, w_out_full[:attn_cols], preferre...]
    another operation x2 -> x0, loops' own time: 38.2 us -> none  [attend(): return lax.map(one_block, jnp.arange(n_blocks))]
    dynamic_slice x32 -> x0, local copies, waits for them, and re-layouts: 31.8 us -> none  [the longest x16 22.6 us: one_block(): q_blk = lax.dynamic_index_in_dim(q_blocks, blk_idx, axis=1, keepdims=False)]
  transfers between devices with their start and end apart: 10 -> 0, of which waited for: 6 -> 0; matrix products, arithmetic and copies ran while one was open for 38% -> 0% of each run, Pallas kernels for 0% -> 0%
where the time goes in v1:
time: 702 us
  Pallas kernels  693 us (99%)
    pallas_call x2, Pallas kernels, project(): pl.pallas_call(kernel, out_shape=out_shape, in_specs=[anywhere] * len(arg...  379 us
    pallas_call x2, Pallas kernels, attend_and_sum(): pl.pallas_call(kernel, out_shape=out_shape, in_specs=[pl.BlockSpec(memory...  313 us

profile of v1, /device:TPU:97, one launch (start us, length us, event | category | flops | bytes accessed | tf_op | source)
XLA Modules:
  0.0 701.9 jit_solution(1202346537370124962)
XLA Ops:
  0.0 1.3 pad_convert_fusion.refs_4_
  1.3 1.1 slice.19
  2.4 2.1 pad_maximum_fusion.refs_1_.refs_7_
  4.5 192.5 %project_0.1 = (bf16[4,2,1024,256]{3,2,1,0:T(8,128)(2,1)}, bf16[4,2,1024,1024]{3,2,1,0:T(8,128)(2,1)}, bf16[8,1024,256]{2,1,0:T(8,128)(2,1)}, f32[4,8,512]{2,1,0...) custom-call(bf16[1024,2048]{1,0:T(8,128)(2,1)} %bitcast.3, ...), custom_call_target="tpu_custom_call" | custom-call | flops 77309411328 | bytes 33554432 | tf_op jit(solution)/shard_map/project_0/pallas_call | solution.py:518
  196.9 176.4 %attend_and_sum_0.1 = (bf16[1024,2048]{1,0:T(8,128)(2,1)}, bf16[1024,2048]{1,0:T(8,128)(2,1)}, bf16[10,4,512,256]{3,2,1,0:T(8,128)(2,1)}) custom-call(s32[8]{0:T(128)} %refs_0_.3, bf16[4,2,1024,256]{3,2,1,0:T(8,128)(2,1)} %get-tuple-element.31.refs_1_, bf16[4,2,1024,1024]{3,2,1,0:T(8,128)(2,1)} %get-tuple-element.32.refs_2_, ...), custom_call_target="tpu_custom_call" | custom-call | flops 42949672960 | bytes 33554432 | tf_op jit(solution)/shard_map/attend_and_sum_0/pallas_call | solution.py:858
  373.4 187.0 %project_1.1 = (bf16[4,2,1024,256]{3,2,1,0:T(8,128)(2,1)}, bf16[4,2,1024,1024]{3,2,1,0:T(8,128)(2,1)}, bf16[8,1024,256]{2,1,0:T(8,128)(2,1)}, bf16[2,1280,256]{2,1,0:T(8,128)(2,1)}, bf16[2,4,1280,256]{3,2,1,0:T(8,128)(2,1)}) custom-call(bf16[1024,2048]{1,0:T(8,128)(2,1)} %get-tuple-element.35.refs_0_.refs_4_, ...), custom_call_target="tpu_custom_call" | custom-call | flops 77309411328 | bytes 33554432 | tf_op jit(solution)/shard_map/project_1/pallas_call | solution.py:518
  560.4 136.7 %attend_and_sum_1.1 = bf16[1024,2048]{1,0:T(8,128)(2,1)} custom-call(s32[8]{0:T(128)} %refs_0_.3, bf16[4,2,1024,256]{3,2,1,0:T(8,128)(2,1)} %get-tuple-element.40.refs_1_, bf16[4,2,1024,1024]{3,2,1,0:T(8,128)(2,1)} %get-tuple-element.41.refs_2_, bf16[8,1024,256]{2,1,0:T(8,128)(2,1)} %get-tuple-element.42.refs_3_, ...), custom_call_target="tpu_custom_call" | custom-call | flops 42949672960 | bytes 33554432 | tf_op jit(solution)/shard_map/attend_and_sum_1/pallas_call | solution.py:858
  697.1 4.8 copy.8

commit v2 on v1

--- a/solution.py
+++ b/solution.py
@@ -12,7 +12,7 @@
 MESH = pl.DeviceIdType.MESH
 BF16, F32 = jnp.bfloat16, jnp.float32
 
-UP, DOWN, FORWARD, FIRST, SIDE_UP, SIDE_DOWN, FAR, MATE, SIDE_MATE, KINDS = 0, 1, 2, 3, 4, 5, 6, 7, 11, 15
+UP, DOWN, FORWARD, FORWARD_B, FIRST, SIDE_UP, SIDE_DOWN, FAR, MATE, SIDE_MATE = range(10)
 
 
 def rms_norm(x_in, gain):
@@ -51,127 +51,181 @@
     )
 
 
-class Gather:
+class GatherIn:
     def __init__(self, place, buf, own, send, recv, local, first=None, column=None):
         self.place, self.buf, self.own, self.first, self.column = place, buf, own, first, column
         self.send, self.recv, self.local = send, recv, local
 
-    def at(self, block, p, slot):
-        return self.buf.at[block, p, slot]
-
-    def _copy(self, src, dst, kind, p, target):
-        return remote(src, dst, self.send.at[kind, p], self.recv.at[kind, p], target)
-
-    def up(self, p):
-        y = self.place.y
-        return self._copy(self.own(p), self.at(0, p, y), UP, p, {"data": self.place.up})
-
-    def down(self, p):
-        y = self.place.y
-        return self._copy(self.own(p), self.at(0, p, y), DOWN, p, {"data": self.place.down})
-
-    def forward(self, p):
-        even = lax.rem(p, 2) == 0
-        slot = jnp.where(even, self.place.down, self.place.up)
+    def at(self, block, g, slot):
+        return self.buf.at[block, g, slot]
+
+    def _copy(self, src, dst, kind, at, target):
+        return remote(src, dst, self.send.at[kind, at], self.recv.at[kind, at], target)
+
+    def up(self, g, half):
+        dst = self.at(0, g, self.place.y).at[half]
+        return self._copy(self.own(g, half), dst, UP, 2 * g + half, {"data": self.place.up})
+
+    def down(self, g, half):
+        dst = self.at(0, g, self.place.y).at[half]
+        return self._copy(self.own(g, half), dst, DOWN, 2 * g + half, {"data": self.place.down})
+
+    def neighbour_first(self, g, half):
+        dst = self.at(2, g, self.place.y).at[half]
+        return self._copy(self.own(g, half), dst, FIRST, 2 * g + half, {"model": self.place.neighbour})
+
+    def forward(self, g):
+        even = lax.rem(g, 2) == 0
+        ref = self.at(0, g, jnp.where(even, self.place.down, self.place.up))
         target = jnp.where(even, self.place.up, self.place.down)
-        return self._copy(self.at(0, p, slot), self.at(0, p, slot), FORWARD, p, {"data": target})
-
-    def neighbour_first(self, p):
-        return self._copy(self.own(p), self.at(2, p, self.place.y), FIRST, p, {"model": self.place.neighbour})
-
-    def _first(self, p):
-        return self.at(2, p, self.place.y) if self.first is None else self.first.at[p]
-
-    def side_up(self, p):
-        return self._copy(self._first(p), self.at(2, p, self.place.y), SIDE_UP, p, {"data": self.place.up})
-
-    def side_down(self, p):
-        return self._copy(self._first(p), self.at(2, p, self.place.y), SIDE_DOWN, p, {"data": self.place.down})
-
-    def neighbour_far(self, p):
-        far = self.place.far
-        src = self.at(0, p, far) if self.column is None else self.column.at[p, far]
-        return self._copy(src, self.at(2, p, far), FAR, p, {"model": self.place.neighbour})
-
-    def mate(self, p, which):
+        return self._copy(ref, ref, FORWARD, g, {"data": target})
+
+    def _side(self, g):
+        return self.at(2, g, self.place.y) if self.first is None else self.first.at[g]
+
+    def side_up(self, g):
+        return self._copy(self._side(g), self.at(2, g, self.place.y), SIDE_UP, g, {"data": self.place.up})
+
+    def side_down(self, g):
+        return self._copy(self._side(g), self.at(2, g, self.place.y), SIDE_DOWN, g, {"data": self.place.down})
+
+    def far(self, g):
+        slot = self.place.far
+        src = self.at(0, g, slot) if self.column is None else self.column.at[g, slot]
+        return self._copy(src, self.at(2, g, slot), FAR, g, {"model": self.place.neighbour})
+
+    def mate(self, g):
+        return self._copy(self.buf.at[0, g], self.buf.at[1, g], MATE, g, {"model": self.place.mate})
+
+    def side_mate(self, g):
+        return self._copy(self.buf.at[2, g], self.buf.at[3, g], SIDE_MATE, g, {"model": self.place.mate})
+
+    def load_own(self, g, half):
+        dst = self.at(0, g, self.place.y).at[half]
+        return pltpu.make_async_copy(self.own(g, half), dst, self.local.at[half, g])
+
+    def load_column(self, g, which):
         slot = self.place.slots[which]
-        if which == 0:
-            src = self.own(p)
-        else:
-            src = self.at(0, p, slot) if self.column is None else self.column.at[p, slot]
-        return self._copy(src, self.at(1, p, slot), MATE + which, p, {"model": self.place.mate})
-
-    def side_mate(self, p, which):
-        slot = self.place.slots[which]
-        src = self._first(p) if which == 0 else self.at(2, p, slot)
-        return self._copy(src, self.at(3, p, slot), SIDE_MATE + which, p, {"model": self.place.mate})
-
-    def load_own(self, p):
-        return pltpu.make_async_copy(self.own(p), self.at(0, p, self.place.y), self.local.at[0, p])
-
-    def load_column(self, p, which):
-        slot = self.place.slots[which]
-        return pltpu.make_async_copy(self.column.at[p, slot], self.at(0, p, slot), self.local.at[which, p])
-
-    def load_first(self, p):
-        return pltpu.make_async_copy(self.first.at[p], self.at(2, p, self.place.y), self.local.at[4, p])
-
-    def pass_side(self, p):
-        self.side_up(p).wait_recv()
-        self.side_mate(p, 1).start()
-        self.side_down(p).wait_recv()
-        self.side_mate(p, 2).start()
-        self.neighbour_far(p).wait_recv()
-        self.side_mate(p, 3).start()
-
-    def wait_sends(self, p):
-        made = [self.side_up(p), self.side_down(p), self.neighbour_far(p)]
+        return pltpu.make_async_copy(self.column.at[g, slot], self.at(0, g, slot), self.local.at[1 + which, g])
+
+    def load_first(self, g):
+        return pltpu.make_async_copy(self.first.at[g], self.at(2, g, self.place.y), self.local.at[5, g])
+
+    def pass_side(self, g):
+        if self.first is not None:
+            self.load_first(g).wait()
+        self.side_up(g).wait_recv()
+        self.side_down(g).wait_recv()
+        self.far(g).wait_recv()
+        self.side_mate(g).start()
+
+    def wait_sends(self, g):
+        made = [self.side_up(g), self.side_down(g), self.far(g), self.mate(g), self.side_mate(g)]
         if self.column is None:
-            made += [self.up(p), self.down(p), self.forward(p)]
+            made += [self.forward(g)] + [copy(g, half) for copy in (self.up, self.down) for half in range(2)]
         if self.first is None:
-            made.append(self.neighbour_first(p))
-        made += [self.mate(p, which) for which in range(4)] + [self.side_mate(p, which) for which in range(4)]
+            made += [self.neighbour_first(g, half) for half in range(2)]
         for copy in made:
             copy.wait_send()
 
 
-class Prefetch:
+class FetchIn:
     def __init__(self, place, own, send, recv, neighbour=None, first=None, column=None):
         self.place, self.own, self.send, self.recv = place, own, send, recv
         self.neighbour, self.first, self.column = neighbour, first, column
 
-    def up(self, p):
-        dst = self.column.at[p, self.place.y]
-        return remote(self.own(p), dst, self.send.at[0, p], self.recv.at[0, p], {"data": self.place.up})
-
-    def down(self, p):
-        dst = self.column.at[p, self.place.y]
-        return remote(self.own(p), dst, self.send.at[1, p], self.recv.at[1, p], {"data": self.place.down})
-
-    def forward(self, p):
-        even = lax.rem(p, 2) == 0
-        slot = jnp.where(even, self.place.down, self.place.up)
+    def _ring(self, g, half, kind, target):
+        at = 2 * g + half
+        dst = self.column.at[g, self.place.y, half]
+        return remote(self.own(g, half), dst, self.send.at[kind, at], self.recv.at[kind, at], {"data": target})
+
+    def up(self, g, half):
+        return self._ring(g, half, 0, self.place.up)
+
+    def down(self, g, half):
+        return self._ring(g, half, 1, self.place.down)
+
+    def forward(self, g):
+        even = lax.rem(g, 2) == 0
+        ref = self.column.at[g, jnp.where(even, self.place.down, self.place.up)]
         target = jnp.where(even, self.place.up, self.place.down)
-        ref = self.column.at[p, slot]
-        return remote(ref, ref, self.send.at[2, p], self.recv.at[2, p], {"data": target})
-
-    def neighbour_first(self, p):
-        return remote(self.own(p), self.first.at[p], self.send.at[3, p], self.recv.at[3, p], {"model": self.neighbour})
-
-
-def in_pieces(layer, head_ref, w_ref, c, ff):
-    def own(p):
-        if isinstance(p, int) and p < 2:
-            return head_ref.at[layer, :, pl.ds(p * c, c)]
-        column = (p // 2) * c + lax.rem(p, 2) * ff
-        return w_ref.at[layer, :, pl.ds(pl.multiple_of(column, c), c)]
-
-    return own
-
-
-def out_pieces(layer, w_ref, width):
-    def own(p):
-        return w_ref.at[layer, :, pl.ds(pl.multiple_of(p * width, width), width)]
+        return remote(ref, ref, self.send.at[2, g], self.recv.at[2, g], {"data": target})
+
+    def neighbour_first(self, g, half):
+        at = 2 * g + half
+        dst = self.first.at[g, half]
+        return remote(self.own(g, half), dst, self.send.at[3, at], self.recv.at[3, at], {"model": self.neighbour})
+
+
+class GatherOut:
+    def __init__(self, place, buf, own, send, recv, local=None, first=None, column=None):
+        self.place, self.buf, self.own, self.first, self.column = place, buf, own, first, column
+        self.send, self.recv, self.local = send, recv, local
+
+    def _copy(self, src, dst, kind, target):
+        return remote(src, dst, self.send.at[kind], self.recv.at[kind], target)
+
+    def up(self):
+        return self._copy(self.own, self.buf.at[0, self.place.y], UP, {"data": self.place.up})
+
+    def down(self):
+        return self._copy(self.own, self.buf.at[0, self.place.y], DOWN, {"data": self.place.down})
+
+    def _half(self, ref, second):
+        size = ref.shape[0] // 2
+        return ref.at[pl.ds(second * size, size)]
+
+    def forward(self):
+        ref = self._half(self.buf.at[0, self.place.down], 0)
+        return self._copy(ref, ref, FORWARD, {"data": self.place.up})
+
+    def forward_b(self):
+        ref = self._half(self.buf.at[0, self.place.up], 1)
+        return self._copy(ref, ref, FORWARD_B, {"data": self.place.down})
+
+    def neighbour_first(self, dst):
+        return self._copy(self.own, dst, FIRST, {"model": self.place.neighbour})
+
+    def side_up(self):
+        return self._copy(self.first, self.buf.at[2, self.place.y], SIDE_UP, {"data": self.place.up})
+
+    def side_down(self):
+        return self._copy(self.first, self.buf.at[2, self.place.y], SIDE_DOWN, {"data": self.place.down})
+
+    def far(self):
+        slot = self.place.far
+        src = self.buf.at[0, slot] if self.column is None else self.column.at[0, slot]
+        return self._copy(src, self.buf.at[2, slot], FAR, {"model": self.place.neighbour})
+
+    def mate(self, which):
+        slot = self.place.slots[which]
+        if which == 0:
+            src = self.own
+        else:
+            src = self.buf.at[0, slot] if self.column is None else self.column.at[0, slot]
+        return self._copy(src, self.buf.at[1, slot], MATE + 2 * which, {"model": self.place.mate})
+
+    def side_mate(self, which):
+        slot = self.place.slots[which]
+        src = self.first if which == 0 else self.buf.at[2, slot]
+        return self._copy(src, self.buf.at[3, slot], SIDE_MATE + 2 * which, {"model": self.place.mate})
+
+    def load_own(self):
+        return pltpu.make_async_copy(self.own, self.buf.at[0, self.place.y], self.local.at[0])
+
+    def load_column(self, which):
+        slot = self.place.slots[which]
+        return pltpu.make_async_copy(self.column.at[0, slot], self.buf.at[0, slot], self.local.at[which])
+
+    def load_first(self):
+        return pltpu.make_async_copy(self.first, self.buf.at[2, self.place.y], self.local.at[4])
+
+
+def in_halves(layer, head_ref, w_ref, c, ff):
+    def own(g, half):
+        if isinstance(g, int) and g == 0:
+            return head_ref.at[layer, :, pl.ds(half * c, c)]
+        return w_ref.at[layer, :, pl.ds(pl.multiple_of(g * c + half * ff, c), c)]
 
     return own
 
@@ -184,8 +238,6 @@
     depth, out_part = w_out.shape[1:]
     ff = depth - c
     n_group = 1 + ff // c
-    pieces = 2 * n_group
-    width = out_part // 2
     n_units = 8 * n_group
     row_parts = 4
     row_part = rows // row_parts
@@ -208,14 +260,12 @@
 
         place = Place(n_data, n_model, partner, neighbour)
         place.meet()
-        w = Gather(place, wbuf, in_pieces(layer, head_ref, w_ref, c, ff), send, recv, w_local, first_ref, column_ref)
-        out_own = out_pieces(layer, wo_ref, width)
+        w = GatherIn(place, wbuf, in_halves(layer, head_ref, w_ref, c, ff), send, recv, w_local, first_ref, column_ref)
+        out_column = None if start_layer else out_column_ref
+        out_next = GatherOut(place, out_column, wo_ref.at[layer], next_send, next_recv)
         if start_layer:
-            out_next = Prefetch(place, out_own, next_send, next_recv, place.neighbour, out_first_ref)
-            in_own = in_pieces(layer + 1, head_ref, w_ref, c, ff)
-            in_next = Prefetch(place, in_own, late_send, late_recv, next_neighbour(place.me), in_first_ref)
-        else:
-            out_next = Prefetch(place, out_own, next_send, next_recv, place.neighbour, out_first_ref, out_column_ref)
+            in_own = in_halves(layer + 1, head_ref, w_ref, c, ff)
+            in_next = FetchIn(place, in_own, late_send, late_recv, next_neighbour(place.me), in_first_ref)
 
         def c_x(part_no):
             piece = pl.ds(part_no * row_part, row_part)
@@ -249,51 +299,43 @@
         load_gain.start()
         load_x.start()
         if start_layer:
-            for p in range(4):
-                w.up(p).start()
-                w.down(p).start()
-            for p in range(pieces):
-                w.neighbour_first(p).start()
-                w.load_own(p).start()
+            for g in range(2):
+                for half in range(2):
+                    w.up(g, half).start()
+                    w.down(g, half).start()
+            for g in range(n_group):
+                for half in range(2):
+                    w.neighbour_first(g, half).start()
+                    w.load_own(g, half).start()
             for part_no in range(row_parts):
                 c_x(part_no).start()
-            for p in range(pieces):
-                w.mate(p, 0).start()
         else:
             load_par.start()
-            for p in range(pieces):
-                w.load_own(p).start()
+            for g in range(n_group):
+                for half in range(2):
+                    w.load_own(g, half).start()
                 for which in range(1, 4):
-                    w.load_column(p, which).start()
-                w.mate(p, 0).start()
-                w.side_up(p).start()
-                w.side_down(p).start()
-                w.neighbour_far(p).start()
-                for which in range(1, 4):
-                    w.mate(p, which).start()
-            for p in range(pieces):
-                w.load_first(p).start()
-                w.side_mate(p, 0).start()
-            for p in range(2):
-                out_next.neighbour_first(p).start()
-                out_next.up(p).start()
-                out_next.down(p).start()
+                    w.load_column(g, which).start()
+                w.side_up(g).start()
+                w.side_down(g).start()
+                w.far(g).start()
+            for g in range(n_group):
+                w.load_first(g).start()
+            out_next.neighbour_first(out_first_ref).start()
+            out_next.up().start()
+            out_next.down().start()
 
         def ring_stage(g):
-            for p in (2 * g, 2 * g + 1):
-                w.up(p).wait_recv()
-                w.down(p).wait_recv()
-                w.forward(p).start()
+            for half in range(2):
+                w.up(g, half).wait_recv()
+                w.down(g, half).wait_recv()
+            w.forward(g).start()
 
             @pl.when(g + 2 < n_group)
             def _():
-                for p in (2 * g + 4, 2 * g + 5):
-                    w.up(p).start()
-                    w.down(p).start()
-
-            for p in (2 * g, 2 * g + 1):
-                w.mate(p, 1).start()
-                w.mate(p, 2).start()
+                for half in range(2):
+                    w.up(g + 2, half).start()
+                    w.down(g + 2, half).start()
 
         if start_layer:
             for which in range(3):
@@ -316,13 +358,19 @@
         if start_layer:
             ring_stage(0)
         else:
+            for g in range(n_group):
+                for half in range(2):
+                    w.load_own(g, half).wait()
+                for which in range(1, 4):
+                    w.load_column(g, which).wait()
+                w.mate(g).start()
             load_par.wait()
 
             @pl.loop(0, row_parts)
             def _(part_no):
                 norm_rows(1, part_no)
 
-        half, quarter = n_units // 2, n_units // 4
+        halfway, quarter = n_units // 2, n_units // 4
 
         def out_copy(slot, blk, side, g):
             def to_q():
@@ -336,11 +384,11 @@
 
         @pl.loop(0, n_units)
         def _(step):
-            late = step - half
+            late = step - halfway
             if start_layer:
-                opening, second = step < quarter, (step >= quarter) & (step < half)
+                opening, second = step < quarter, (step >= quarter) & (step < halfway)
                 g = jnp.where(opening, step // 2, jnp.where(second, (step - quarter) // 2, late // 4))
-                blk = jnp.where(step < half, lax.rem(step, 2), 2 + lax.rem(late, 4) // 2)
+                blk = jnp.where(step < halfway, lax.rem(step, 2), 2 + lax.rem(late, 4) // 2)
                 side = jnp.where(opening, 0, jnp.where(second, 1, lax.rem(late, 2)))
 
                 @pl.when(opening & (blk == 0))
@@ -351,24 +399,22 @@
 
                     @pl.when(g + 2 == n_group)
                     def _():
-                        @pl.loop(0, pieces)
-                        def _(p):
-                            w.neighbour_first(p).wait_recv()
-                            w.side_up(p).start()
-                            w.side_down(p).start()
-                            w.side_mate(p, 0).start()
-
-                    for p in (2 * g, 2 * g + 1):
-                        w.forward(p).wait_recv()
-                        w.mate(p, 3).start()
-                        w.neighbour_far(p).start()
-                        w.load_own(p).wait()
+                        @pl.loop(0, n_group)
+                        def _(k):
+                            for half in range(2):
+                                w.neighbour_first(k, half).wait_recv()
+                            w.side_up(k).start()
+                            w.side_down(k).start()
+
+                    w.forward(g).wait_recv()
+                    w.far(g).start()
+                    for half in range(2):
+                        w.load_own(g, half).wait()
+                    w.mate(g).start()
 
                 @pl.when(opening & (blk == 1))
                 def _():
-                    for p in (2 * g, 2 * g + 1):
-                        for which in range(4):
-                            w.mate(p, which).wait_recv()
+                    w.mate(g).wait_recv()
 
                 @pl.when(step == quarter)
                 def _():
@@ -377,56 +423,37 @@
                         c_x(part_no).wait_recv()
                         norm_rows(1, part_no)
 
-                    for p in range(2):
-                        out_next.neighbour_first(p).start()
-                    for p in range(pieces):
-                        in_next.neighbour_first(p).start()
+                    out_next.neighbour_first(out_first_ref).start()
+                    for k in range(n_group):
+                        for half in range(2):
+                            in_next.neighbour_first(k, half).start()
             else:
                 g = jnp.where(late < 0, step, late) // 4
                 blk = jnp.where(late < 0, 0, 2) + lax.rem(step, 4) // 2
                 side = lax.rem(step, 2)
 
-                @pl.when((late < 0) & (lax.rem(step, 4) == 0))
-                def _():
-                    for p in (2 * g, 2 * g + 1):
-                        w.load_own(p).wait()
-                        for which in range(1, 4):
-                            w.load_column(p, which).wait()
-
                 @pl.when((late < 0) & (lax.rem(step, 4) == 2))
                 def _():
-                    for p in (2 * g, 2 * g + 1):
-                        for which in range(4):
-                            w.mate(p, which).wait_recv()
-
-                @pl.when(step == half - 2)
+                    w.mate(g).wait_recv()
+
+                @pl.when(step == n_units - 6)
                 def _():
-                    @pl.loop(0, pieces)
-                    def _(p):
-                        w.load_first(p).wait()
-
-                @pl.when(step == n_units - 4)
-                def _():
-                    for p in range(2):
-                        out_next.up(p).wait_recv()
-                        out_next.down(p).wait_recv()
-                        out_next.forward(p).start()
-
-            @pl.when(step == half - 2)
-            def _():
-                for p in range(2):
-                    w.pass_side(p)
+                    out_next.up().wait_recv()
+                    out_next.down().wait_recv()
+                    out_next.forward().start()
+                    out_next.forward_b().start()
+
+            @pl.when(step == halfway - 2)
+            def _():
+                w.pass_side(0)
 
             @pl.when((late >= 0) & (lax.rem(late, 4) == 2))
             def _():
                 @pl.when(g + 1 < n_group)
                 def _():
-                    for p in (2 * g + 2, 2 * g + 3):
-                        w.pass_side(p)
-
-                for p in (2 * g, 2 * g + 1):
-                    for which in range(4):
-                        w.side_mate(p, which).wait_recv()
+                    w.pass_side(g + 1)
+
+                w.side_mate(g).wait_recv()
 
             slot = lax.rem(step, 2)
             to_q, to_m = out_copy(slot, blk, side, g)
@@ -435,8 +462,8 @@
             def _():
                 to_q().wait()
 
-            def columns(p):
-                return wbuf[blk, p].reshape(d_model, c)
+            def columns(half):
+                return wbuf[blk, g, :, half].reshape(d_model, c)
 
             @pl.when(g == 0)
             def _():
@@ -447,8 +474,8 @@
             @pl.when(g > 0)
             def _():
                 h_val = h_ref[side]
-                gate = jnp.dot(h_val, columns(2 * g), preferred_element_type=F32).astype(BF16).astype(F32)
-                raised = jnp.dot(h_val, columns(2 * g + 1), preferred_element_type=F32).astype(BF16).astype(F32)
+                gate = jnp.dot(h_val, columns(0), preferred_element_type=F32).astype(BF16).astype(F32)
+                raised = jnp.dot(h_val, columns(1), preferred_element_type=F32).astype(BF16).astype(F32)
                 stage[slot] = (gate * jax.nn.sigmoid(gate) * raised).astype(BF16)
                 to_m().start()
 
@@ -480,21 +507,21 @@
                 c_gain(which).wait_send()
             for part_no in range(row_parts):
                 c_x(part_no).wait_send()
-            for p in range(pieces):
-                in_next.neighbour_first(p).wait()
+            for g in range(n_group):
+                for half in range(2):
+                    in_next.neighbour_first(g, half).wait()
         else:
-            for p in range(2):
-                out_next.forward(p).wait()
-                out_next.up(p).wait_send()
-                out_next.down(p).wait_send()
-        for p in range(2):
-            out_next.neighbour_first(p).wait()
+            for copy in (out_next.forward(), out_next.forward_b()):
+                copy.wait()
+            for copy in (out_next.up(), out_next.down()):
+                copy.wait_send()
+        out_next.neighbour_first(out_first_ref).wait()
         for slot in range(2):
             pltpu.make_async_copy(stage.at[slot], q_ref.at[0, 0], out_sem.at[slot]).wait()
 
-        @pl.loop(0, pieces)
-        def _(p):
-            w.wait_sends(p)
+        @pl.loop(0, n_group)
+        def _(g):
+            w.wait_sends(g)
 
     anywhere = pl.BlockSpec(memory_space=pl.ANY)
     out_shape = [
@@ -505,13 +532,13 @@
     if start_layer:
         out_shape += [
             jax.ShapeDtypeStruct(gain_shape, F32),
-            jax.ShapeDtypeStruct((2, depth, width), BF16),
-            jax.ShapeDtypeStruct((pieces, part, c), BF16),
+            jax.ShapeDtypeStruct((depth, out_part), BF16),
+            jax.ShapeDtypeStruct((n_group, 2, part, c), BF16),
         ]
     else:
         out_shape += [
-            jax.ShapeDtypeStruct((2, depth, width), BF16),
-            jax.ShapeDtypeStruct((2, n_data, depth, width), BF16),
+            jax.ShapeDtypeStruct((depth, out_part), BF16),
+            jax.ShapeDtypeStruct((1, n_data, depth, out_part), BF16),
         ]
     dma = pltpu.SemaphoreType.DMA
     args = (x_own, head, w_in, w_out) + tuple(extra)
@@ -521,13 +548,13 @@
         in_specs=[anywhere] * len(args),
         out_specs=[anywhere] * len(out_shape),
         scratch_shapes=[
-            pltpu.VMEM((4, pieces, n_data, part, c), BF16),
+            pltpu.VMEM((4, n_group, n_data, 2, part, c), BF16),
             pltpu.VMEM((2, rows, d_model), BF16),
             pltpu.VMEM(gain_shape, F32),
             pltpu.VMEM((2, rows, c), BF16),
             pltpu.VMEM((rows, c), BF16),
-            dma((KINDS, pieces)), dma((KINDS, pieces)), dma((5, pieces)),
-            dma((4, 2)), dma((4, 2)), dma((4, pieces)), dma((4, pieces)),
+            dma((SIDE_MATE + 1, 2 * n_group)), dma((SIDE_MATE + 1, 2 * n_group)), dma((6, n_group)),
+            dma((FIRST + 1,)), dma((FIRST + 1,)), dma((4, 2 * n_group)), dma((4, 2 * n_group)),
             dma((row_parts,)), dma((row_parts,)), dma((3,)), dma((3,)),
             dma((n_model - 1,)), dma((n_model - 1,)), dma((3,)), dma((2,)),
         ],
@@ -542,7 +569,6 @@
     ff = m.shape[3]
     d_model = x_own.shape[1]
     depth, out_part = w_out.shape[1:]
-    width = out_part // 2
     head_dim = c // 2
     n_batch = lens.shape[0]
     slab_len = rows // n_batch
@@ -555,7 +581,7 @@
     key_rows = 2 * slab_len
     scale = head_dim ** -0.5 * 1.4426950408889634
     part = head.shape[1]
-    in_count = 2 * (1 + ff // c)
+    n_group = 1 + ff // c
     ready = column is not None
     held = tiles // 2
 
@@ -579,7 +605,7 @@
 
         place = Place(n_data, n_model, partner, neighbour)
         place.meet()
-        w = Gather(place, wbuf, out_pieces(layer, wo_ref, width), send, recv, w_local, first_ref, column_ref)
+        w = GatherOut(place, wbuf, wo_ref.at[layer], send, recv, w_local, first_ref, column_ref)
 
         def tile_of(k):
             which = k // chunks
@@ -619,25 +645,23 @@
         load_q.start()
         load_kv.start()
         load_m(0).start()
-        for p in range(2):
-            w.load_own(p).start()
-            w.load_first(p).start()
-            w.mate(p, 0).start()
-            w.side_mate(p, 0).start()
-        for p in range(2):
-            if ready:
-                for which in range(1, 4):
-                    w.load_column(p, which).start()
-                    w.mate(p, which).start()
-                w.neighbour_far(p).start()
-            else:
-                w.up(p).start()
-                w.down(p).start()
-        for p in range(2):
-            w.side_up(p).start()
-            w.side_down(p).start()
+        w.load_own().start()
+        w.load_first().start()
+        w.mate(0).start()
+        w.side_mate(0).start()
+        if ready:
+            w.far().start()
+            for which in range(1, 4):
+                w.load_column(which).start()
+                w.mate(which).start()
+        else:
+            w.up().start()
+            w.down().start()
+        w.side_up().start()
+        w.side_down().start()
         if not last:
-            in_next = Prefetch(place, in_pieces(layer + 1, head_ref, wi_ref, c, ff), in_send, in_recv, column=in_column_ref)
+            in_own = in_halves(layer + 1, head_ref, wi_ref, c, ff)
+            in_next = FetchIn(place, in_own, in_send, in_recv, column=in_column_ref)
 
         @pl.loop(0, tiles)
         def _(k):
@@ -718,69 +742,65 @@
 
             @pl.when(step == 0)
             def _():
-                for p in range(2):
-                    w.load_own(p).wait()
-                    w.load_first(p).wait()
-                    w.mate(p, 0).wait_recv()
-                    w.side_mate(p, 0).wait_recv()
+                w.load_own().wait()
+                w.load_first().wait()
+                w.mate(0).wait_recv()
+                w.side_mate(0).wait_recv()
 
             if not ready:
 
                 @pl.when(step == 2)
                 def _():
-                    for p in range(2):
-                        w.up(p).wait_recv()
-                        w.down(p).wait_recv()
-                        w.forward(p).start()
-                        w.mate(p, 1).start()
-                        w.mate(p, 2).start()
+                    w.up().wait_recv()
+                    w.down().wait_recv()
+                    w.forward().start()
+                    w.forward_b().start()
+                    w.mate(1).start()
+                    w.mate(2).start()
                     if not last:
-                        for p in range(4):
-                            in_next.up(p).start()
-                            in_next.down(p).start()
+                        for g in range(2):
+                            for half in range(2):
+                                in_next.up(g, half).start()
+                                in_next.down(g, half).start()
 
                 @pl.when(step == chunks + 2)
                 def _():
-                    for p in range(2):
-                        w.forward(p).wait_recv()
-                        w.mate(p, 3).start()
-                        w.neighbour_far(p).start()
+                    w.forward().wait_recv()
+                    w.forward_b().wait_recv()
+                    w.far().start()
+                    w.mate(3).start()
 
             @pl.when(step == chunks)
             def _():
-                for p in range(2):
-                    w.side_up(p).wait_recv()
-                    w.side_mate(p, 1).start()
-                    w.side_down(p).wait_recv()
-                    w.side_mate(p, 2).start()
-                for p in range(2):
-                    for one in (1, 2):
-                        if ready:
-                            w.load_column(p, one).wait()
-                        w.mate(p, one).wait_recv()
-                        w.side_mate(p, one).wait_recv()
+                w.side_up().wait_recv()
+                w.side_mate(1).start()
+                w.side_down().wait_recv()
+                w.side_mate(2).start()
+                for one in (1, 2):
+                    if ready:
+                        w.load_column(one).wait()
+                    w.mate(one).wait_recv()
+                    w.side_mate(one).wait_recv()
 
             @pl.when(step == 3 * chunks)
             def _():
-                for p in range(2):
-                    w.neighbour_far(p).wait_recv()
-                    w.side_mate(p, 3).start()
-                for p in range(2):
-                    if ready:
-                        w.load_column(p, 3).wait()
-                    w.mate(p, 3).wait_recv()
-                    w.side_mate(p, 3).wait_recv()
+                w.far().wait_recv()
+                w.side_mate(3).start()
+                if ready:
+                    w.load_column(3).wait()
+                w.mate(3).wait_recv()
+                w.side_mate(3).wait_recv()
 
             if not last:
                 @pl.when((step >= chunks + 3) & (lax.rem(step, 2) == 1))
                 def _():
                     g = (step - chunks - 3) // 2
 
-                    @pl.when(g < in_count // 2 - 2)
+                    @pl.when(g < n_group - 2)
                     def _():
-                        for p in (2 * g + 4, 2 * g + 5):
-                            in_next.up(p).start()
-                            in_next.down(p).start()
+                        for half in range(2):
+                            in_next.up(g + 2, half).start()
+                            in_next.down(g + 2, half).start()
 
             @pl.when(step >= 4)
             def _():
@@ -789,17 +809,16 @@
             load_m(step).wait()
             here = lax.rem(step, 2)
             rows_c = pl.ds(pl.multiple_of(chunk * crow, crow), crow)
-            for p in range(2):
-                total = None
-                for blk in range(n_blocks):
-                    mid = mbuf[here, blk].reshape(2 * crow, ff)
-                    attn = obuf[blk, :, rows_c, :].reshape(2 * crow, c)
-                    one = jnp.dot(mid, wbuf[blk, p, slot, c:, :], preferred_element_type=F32)
-                    one = one + jnp.dot(attn, wbuf[blk, p, slot, :c, :], preferred_element_type=F32)
-                    total = one if total is None else total + one
-                z = total.astype(BF16)
-                zb[chunk, slot, :, p * width:(p + 1) * width] = z[:crow]
-                z_stage[lax.rem(step, 4), :, p * width:(p + 1) * width] = z[crow:]
+            total = None
+            for blk in range(n_blocks):
+                mid = mbuf[here, blk].reshape(2 * crow, ff)
+                attn = obuf[blk, :, rows_c, :].reshape(2 * crow, c)
+                one = jnp.dot(mid, wbuf[blk, slot, c:, :], preferred_element_type=F32)
+                one = one + jnp.dot(attn, wbuf[blk, slot, :c, :], preferred_element_type=F32)
+                total = one if total is None else total + one
+            z = total.astype(BF16)
+            zb[chunk, slot] = z[:crow]
+            z_stage[lax.rem(step, 4)] = z[crow:]
             c_z(step).start()
 
             early = (step >= 1) & (step <= chunks)
@@ -811,11 +830,12 @@
 
         if not last:
 
-            @pl.loop(0, in_count)
-            def _(p):
-                in_next.up(p).wait_recv()
-                in_next.down(p).wait_recv()
-                in_next.forward(p).start()
+            @pl.loop(0, n_group)
+            def _(g):
+                for half in range(2):
+                    in_next.up(g, half).wait_recv()
+                    in_next.down(g, half).wait_recv()
+                in_next.forward(g).start()
 
         @pl.loop(held, tiles)
         def _(k):
@@ -831,15 +851,20 @@
         def _(k):
             c_z(k).wait_send()
 
-        for p in range(2):
-            w.wait_sends(p)
+        made = [w.side_up(), w.side_down(), w.far()]
+        made += [w.mate(which) for which in range(4)] + [w.side_mate(which) for which in range(4)]
+        if not ready:
+            made += [w.up(), w.down(), w.forward(), w.forward_b()]
+        for copy in made:
+            copy.wait_send()
         if not last:
 
-            @pl.loop(0, in_count)
-            def _(p):
-                in_next.forward(p).wait()
-                in_next.up(p).wait_send()
-                in_next.down(p).wait_send()
+            @pl.loop(0, n_group)
+            def _(g):
+                in_next.forward(g).wait()
+                for half in range(2):
+                    in_next.up(g, half).wait_send()
+                    in_next.down(g, half).wait_send()
 
     anywhere = pl.BlockSpec(memory_space=pl.ANY)
     args = [lens, q, m, kv, x_own, w_out, first]
@@ -851,7 +876,7 @@
     if not last:
         out_shape += [
             jax.ShapeDtypeStruct((rows, d_model), BF16),
-            jax.ShapeDtypeStruct((in_count, n_data, part, c), BF16),
+            jax.ShapeDtypeStruct((n_group, n_data, 2, part, c), BF16),
         ]
     dma = pltpu.SemaphoreType.DMA
     tile = (chunks, n_data, crow, out_part)
@@ -861,7 +886,7 @@
         in_specs=[pl.BlockSpec(memory_space=pltpu.SMEM)] + [anywhere] * (len(args) - 1),
         out_specs=[anywhere] * len(out_shape),
         scratch_shapes=[
-            pltpu.VMEM((n_blocks, 2, n_data, depth, width), BF16),
+            pltpu.VMEM((n_blocks, n_data, depth, out_part), BF16),
             pltpu.VMEM(q.shape, BF16),
             pltpu.VMEM(kv.shape, BF16),
             pltpu.VMEM((2, n_blocks, 2, crow, ff), BF16),
@@ -873,7 +898,7 @@
             pltpu.VMEM((qrows, slab_len), F32),
             pltpu.VMEM((qrows, slab_len), F32),
             pltpu.VMEM((qrows, head_dim), F32),
-            dma((KINDS, 2)), dma((KINDS, 2)), dma((5, 2)), dma((4, in_count)), dma((4, in_count)),
+            dma((SIDE_MATE + 7,)), dma((SIDE_MATE + 7,)), dma((5,)), dma((3, 2 * n_group)), dma((3, 2 * n_group)),
             dma((tiles,)), dma((tiles,)), dma((tiles,)), dma((tiles,)), dma((tiles,)), dma((tiles,)), dma((2,)), dma((2,)),
         ],
         compiler_params=pltpu.CompilerParams(collective_id=2 * layer + 1, has_side_effects=True, vmem_limit_bytes=VMEM_LIMIT),

time: 702 us -> 692 us (0.986)
  Pallas kernels: 693 us -> 683 us
    pallas_call x2, Pallas kernels: 379 us -> 371 us  [project(): pl.pallas_call(kernel, out_shape=out_shape, in_specs=[anywhere] * len(arg...]
where the time goes in v2:
time: 692 us
  Pallas kernels  683 us (99%)
    pallas_call x2, Pallas kernels, project(): pl.pallas_call(kernel, out_shape=out_shape, in_specs=[anywhere] * len(arg...  371 us
    pallas_call x2, Pallas kernels, attend_and_sum(): pl.pallas_call(kernel, out_shape=out_shape, in_specs=[pl.BlockSpec(memory...  312 us

profile of v2, /device:TPU:97, one launch (start us, length us, event | category | flops | bytes accessed | tf_op | source)
XLA Modules:
  0.0 692.0 jit_solution(4517649990886477230)
XLA Ops:
  0.0 1.3 pad_convert_fusion.refs_4_
  1.3 1.1 slice.19
  2.4 2.1 pad_maximum_fusion.refs_1_.refs_7_
  4.5 190.5 %project_0.1 = (bf16[4,2,1024,256]{3,2,1,0:T(8,128)(2,1)}, bf16[4,2,1024,1024]{3,2,1,0:T(8,128)(2,1)}, bf16[8,1024,256]{2,1,0:T(8,128)(2,1)}, f32[4,8,512]{2,1,0...) custom-call(bf16[1024,2048]{1,0:T(8,128)(2,1)} %bitcast.3, ...), custom_call_target="tpu_custom_call" | custom-call | flops 77309411328 | bytes 33554432 | tf_op jit(solution)/shard_map/project_0/pallas_call | solution.py:545
  195.0 176.0 %attend_and_sum_0.1 = (bf16[1024,2048]{1,0:T(8,128)(2,1)}, bf16[1024,2048]{1,0:T(8,128)(2,1)}, bf16[5,4,2,512,256]{4,3,2,1,0:T(8,128)(2,1)}) custom-call(s32[8]{0:T(128)} %refs_0_.3, bf16[4,2,1024,256]{3,2,1,0:T(8,128)(2,1)} %get-tuple-element.31.refs_1_, bf16[4,2,1024,1024]{3,2,1,0:T(8,128)(2,1)} %get-tuple-element.32.refs_2_, ...), custom_call_target="tpu_custom_call" | custom-call | flops 42949672960 | bytes 33554432 | tf_op jit(solution)/shard_map/attend_and_sum_0/pallas_call | solution.py:883
  371.0 180.6 %project_1.1 = (bf16[4,2,1024,256]{3,2,1,0:T(8,128)(2,1)}, bf16[4,2,1024,1024]{3,2,1,0:T(8,128)(2,1)}, bf16[8,1024,256]{2,1,0:T(8,128)(2,1)}, bf16[1280,512]{1,0:T(8,128)(2,1)}, bf16[1,4,1280,512]{3,2,1,0:T(8,128)(2,1)}) custom-call(bf16[1024,2048]{1,0:T(8,128)(2,1)} %get-tuple-element.35.refs_0_.refs_4_, ...), custom_call_target="tpu_custom_call" | custom-call | flops 77309411328 | bytes 33554432 | tf_op jit(solution)/shard_map/project_1/pallas_call | solution.py:545
  551.6 135.6 %attend_and_sum_1.1 = bf16[1024,2048]{1,0:T(8,128)(2,1)} custom-call(s32[8]{0:T(128)} %refs_0_.3, bf16[4,2,1024,256]{3,2,1,0:T(8,128)(2,1)} %get-tuple-element.40.refs_1_, bf16[4,2,1024,1024]{3,2,1,0:T(8,128)(2,1)} %get-tuple-element.41.refs_2_, bf16[8,1024,256]{2,1,0:T(8,128)(2,1)} %get-tuple-element.42.refs_3_, ...), custom_call_target="tpu_custom_call" | custom-call | flops 42949672960 | bytes 33554432 | tf_op jit(solution)/shard_map/attend_and_sum_1/pallas_call | solution.py:883
  687.2 4.8 copy.8

commit v3 on v2

--- a/solution.py
+++ b/solution.py
@@ -232,8 +232,9 @@
 
 def project(layer, n_data, n_model, partner, neighbour, next_neighbour, x_own, head, w_in, w_out, extra):
     start_layer = layer == 0
-    rows, d_model = x_own.shape
     part, two_c = head.shape[1:]
+    d_model = part * n_data
+    rows = x_own.size // d_model
     c = two_c // 2
     depth, out_part = w_out.shape[1:]
     ff = depth - c
@@ -243,6 +244,7 @@
     row_part = rows // row_parts
     n_other = n_model // 2 - 1
     gain_shape = (n_data, 8, part)
+    n_tiles = 1 if start_layer else x_own.shape[0] * x_own.shape[1]
 
     def kernel(*refs):
         x_ref, head_ref, w_ref, wo_ref = refs[:4]
@@ -256,7 +258,7 @@
             q_ref, m_ref, kv_ref, out_first_ref, out_column_ref = refs[8:13]
             rest = refs[13:]
         wbuf, h_ref, gbuf, stage, kv_stage, send, recv, w_local, next_send, next_recv, late_send, late_recv = rest[:12]
-        x_send, x_recv, g_send, g_recv, kv_send, kv_recv, local, out_sem = rest[12:]
+        x_send, x_recv, g_send, g_recv, kv_send, kv_recv, local, out_sem, tile_sem = rest[12:]
 
         place = Place(n_data, n_model, partner, neighbour)
         place.meet()
@@ -287,7 +289,15 @@
             return remote(ref, ref, kv_send.at[at], kv_recv.at[at], {"model": place.mate})
 
         save_kv = pltpu.make_async_copy(kv_stage, kv_ref.at[place.me], local.at[0])
-        load_x = pltpu.make_async_copy(x_ref, h_ref.at[0], local.at[0])
+        if start_layer:
+            load_x = pltpu.make_async_copy(x_ref, h_ref.at[0], local.at[0])
+
+        def load_tile(side, k):
+            chunk, slot = k // n_data, lax.rem(k, n_data)
+            src = (x_ref, par_ref)[side].at[chunk, slot]
+            height, across = src.shape
+            down_to, along = pl.multiple_of(chunk * height, height), pl.multiple_of(slot * across, across)
+            return pltpu.make_async_copy(src, h_ref.at[side, pl.ds(down_to, height), pl.ds(along, across)], tile_sem.at[side, k])
 
         if start_layer:
             load_gain = pltpu.make_async_copy(gain_ref, gbuf.at[place.y], local.at[1])
@@ -295,9 +305,16 @@
                 c_gain(which).start()
         else:
             load_gain = pltpu.make_async_copy(gain_ref, gbuf, local.at[1])
-            load_par = pltpu.make_async_copy(par_ref, h_ref.at[1], local.at[2])
         load_gain.start()
-        load_x.start()
+        if start_layer:
+            load_x.start()
+        else:
+            for side in range(2):
+
+                @pl.loop(0, n_tiles)
+                def _(k):
+                    load_tile(side, k).start()
+
         if start_layer:
             for g in range(2):
                 for half in range(2):
@@ -310,7 +327,6 @@
             for part_no in range(row_parts):
                 c_x(part_no).start()
         else:
-            load_par.start()
             for g in range(n_group):
                 for half in range(2):
                     w.load_own(g, half).start()
@@ -345,7 +361,13 @@
         if start_layer:
             save_gain = pltpu.make_async_copy(gbuf, gains_ref, local.at[1])
             save_gain.start()
-        load_x.wait()
+        if start_layer:
+            load_x.wait()
+        else:
+
+            @pl.loop(0, n_tiles)
+            def _(k):
+                load_tile(0, k).wait()
 
         def norm_rows(side, part_no):
             piece = pl.ds(part_no * row_part, row_part)
@@ -364,7 +386,10 @@
                 for which in range(1, 4):
                     w.load_column(g, which).wait()
                 w.mate(g).start()
-            load_par.wait()
+
+            @pl.loop(0, n_tiles)
+            def _(k):
+                load_tile(1, k).wait()
 
             @pl.loop(0, row_parts)
             def _(part_no):
@@ -377,8 +402,7 @@
                 return pltpu.make_async_copy(stage.at[slot], q_ref.at[blk, side], out_sem.at[slot])
 
             def to_m():
-                column = pl.ds(pl.multiple_of((g - 1) * c, c), c)
-                return pltpu.make_async_copy(stage.at[slot], m_ref.at[blk, side, :, column], out_sem.at[slot])
+                return pltpu.make_async_copy(stage.at[slot], m_ref.at[blk, side, g - 1], out_sem.at[slot])
 
             return to_q, to_m
 
@@ -526,7 +550,7 @@
     anywhere = pl.BlockSpec(memory_space=pl.ANY)
     out_shape = [
         jax.ShapeDtypeStruct((4, 2, rows, c), BF16),
-        jax.ShapeDtypeStruct((4, 2, rows, ff), BF16),
+        jax.ShapeDtypeStruct((4, 2, n_group - 1, rows, c), BF16),
         jax.ShapeDtypeStruct((n_model, rows, c), BF16),
     ]
     if start_layer:
@@ -556,7 +580,7 @@
             dma((SIDE_MATE + 1, 2 * n_group)), dma((SIDE_MATE + 1, 2 * n_group)), dma((6, n_group)),
             dma((FIRST + 1,)), dma((FIRST + 1,)), dma((4, 2 * n_group)), dma((4, 2 * n_group)),
             dma((row_parts,)), dma((row_parts,)), dma((3,)), dma((3,)),
-            dma((n_model - 1,)), dma((n_model - 1,)), dma((3,)), dma((2,)),
+            dma((n_model - 1,)), dma((n_model - 1,)), dma((3,)), dma((2,)), dma((2, n_tiles)),
         ],
         compiler_params=pltpu.CompilerParams(collective_id=2 * layer, has_side_effects=True, vmem_limit_bytes=VMEM_LIMIT),
         cost_estimate=pl.CostEstimate(flops=4 * rows * d_model * 4 * (c + 2 * ff), bytes_accessed=16 * rows * d_model, transcendentals=0),
@@ -566,8 +590,10 @@
 
 def attend_and_sum(layer, last, n_data, n_model, partner, neighbour, next_partner, lens, q, m, kv, x_own, w_in, w_out, head, first, column):
     n_blocks, _, rows, c = q.shape
-    ff = m.shape[3]
-    d_model = x_own.shape[1]
+    n_mid = m.shape[2]
+    ff = n_mid * c
+    d_model = w_out.shape[2] * n_data
+    tiled = x_own.ndim == 4
     depth, out_part = w_out.shape[1:]
     head_dim = c // 2
     n_batch = lens.shape[0]
@@ -622,12 +648,13 @@
             chunk, _, _ = tile_of(k)
             slot = lax.rem(k, 2)
             return pltpu.make_async_copy(
-                m_ref.at[:, :, pl.ds(pl.multiple_of(chunk * crow, crow), crow)], mbuf.at[slot], m_sem.at[slot]
+                m_ref.at[:, :, :, pl.ds(pl.multiple_of(chunk * crow, crow), crow)], mbuf.at[slot], m_sem.at[slot]
             )
 
         def load_x(k):
             chunk, _, slot = tile_of(k)
-            return pltpu.make_async_copy(whole(x_ref, chunk, slot), xb.at[chunk, slot], x_sem.at[k])
+            src = x_ref.at[chunk, slot] if tiled else whole(x_ref, chunk, slot)
+            return pltpu.make_async_copy(src, xb.at[chunk, slot], x_sem.at[k])
 
         def c_z(k):
             chunk, _, slot = tile_of(k)
@@ -636,11 +663,12 @@
         def c_y(k):
             chunk, _, slot = tile_of(k)
             target = {"model": next_partner(place.me)}
-            return remote(xb.at[chunk, slot], whole(par_ref, chunk, slot), y_send.at[k], y_recv.at[k], target)
+            return remote(xb.at[chunk, slot], par_ref.at[chunk, slot], y_send.at[k], y_recv.at[k], target)
 
         def save_y(k):
             chunk, _, slot = tile_of(k)
-            return pltpu.make_async_copy(xb.at[chunk, slot], whole(y_ref, chunk, slot), y_save.at[k])
+            dst = whole(y_ref, chunk, slot) if last else y_ref.at[chunk, slot]
+            return pltpu.make_async_copy(xb.at[chunk, slot], dst, y_save.at[k])
 
         load_q.start()
         load_kv.start()
@@ -811,7 +839,7 @@
             rows_c = pl.ds(pl.multiple_of(chunk * crow, crow), crow)
             total = None
             for blk in range(n_blocks):
-                mid = mbuf[here, blk].reshape(2 * crow, ff)
+                mid = jnp.concatenate([mbuf[here, blk, :, k].reshape(2 * crow, c) for k in range(n_mid)], axis=1)
                 attn = obuf[blk, :, rows_c, :].reshape(2 * crow, c)
                 one = jnp.dot(mid, wbuf[blk, slot, c:, :], preferred_element_type=F32)
                 one = one + jnp.dot(attn, wbuf[blk, slot, :c, :], preferred_element_type=F32)
@@ -872,14 +900,14 @@
         args.append(column)
     if not last:
         args += [head, w_in]
-    out_shape = [jax.ShapeDtypeStruct((rows, d_model), BF16)]
+    tile = (chunks, n_data, crow, out_part)
+    out_shape = [jax.ShapeDtypeStruct((rows, d_model) if last else tile, BF16)]
     if not last:
         out_shape += [
-            jax.ShapeDtypeStruct((rows, d_model), BF16),
+            jax.ShapeDtypeStruct(tile, BF16),
             jax.ShapeDtypeStruct((n_group, n_data, 2, part, c), BF16),
         ]
     dma = pltpu.SemaphoreType.DMA
-    tile = (chunks, n_data, crow, out_part)
     return pl.pallas_call(
         kernel,
         out_shape=out_shape,
@@ -889,7 +917,7 @@
             pltpu.VMEM((n_blocks, n_data, depth, out_part), BF16),
             pltpu.VMEM(q.shape, BF16),
             pltpu.VMEM(kv.shape, BF16),
-            pltpu.VMEM((2, n_blocks, 2, crow, ff), BF16),
+            pltpu.VMEM((2, n_blocks, 2, n_mid, crow, c), BF16),
             pltpu.VMEM(tile, BF16),
             pltpu.VMEM(tile, BF16),
             pltpu.VMEM(tile, BF16),

time: 692 us -> 693 us (level)
  no operation moved by 1% of the time
where the time goes in v3:
time: 693 us
  Pallas kernels  684 us (99%)
    pallas_call x2, Pallas kernels, project(): pl.pallas_call(kernel, out_shape=out_shape, in_specs=[anywhere] * len(arg...  372 us
    pallas_call x2, Pallas kernels, attend_and_sum(): pl.pallas_call(kernel, out_shape=out_shape, in_specs=[pl.BlockSpec(memory...  312 us

profile of v3, /device:TPU:97, one launch (start us, length us, event | category | flops | bytes accessed | tf_op | source)
XLA Modules:
  0.0 692.8 jit_solution(7387897333187380544)
XLA Ops:
  0.0 1.3 pad_convert_fusion.refs_4_
  1.3 1.1 slice.19
  2.4 2.1 pad_maximum_fusion.refs_1_.refs_7_
  4.5 190.6 %project_0.1 = (bf16[4,2,1024,256]{3,2,1,0:T(8,128)(2,1)}, bf16[4,2,4,1024,256]{4,3,2,1,0:T(8,128)(2,1)}, bf16[8,1024,256]{2,1,0:T(8,128)(2,1)}, f32[4,8,512]{2,...) custom-call(bf16[1024,2048]{1,0:T(8,128)(2,1)} %bitcast.3, ...), custom_call_target="tpu_custom_call" | custom-call | flops 77309411328 | bytes 33554432 | tf_op jit(solution)/shard_map/project_0/pallas_call | solution.py:569
  195.0 176.1 %attend_and_sum_0.1 = (bf16[4,4,256,512]{3,2,1,0:T(8,128)(2,1)}, bf16[4,4,256,512]{3,2,1,0:T(8,128)(2,1)}, bf16[5,4,2,512,256]{4,3,2,1,0:T(8,128)(2,1)}) custom-call(s32[8]{0:T(128)} %refs_0_.3, bf16[4,2,1024,256]{3,2,1,0:T(8,128)(2,1)} %get-tuple-element.31.refs_1_, bf16[4,2,4,1024,256]{4,3,2,1,0:T(8,128)(2,1)} %get-tuple-element.32.refs_2_, ...), custom_call_target="tpu_custom_call" | custom-call | flops 42949672960 | bytes 33554432 | tf_op jit(solution)/shard_map/attend_and_sum_0/pallas_call | solution.py:911
  371.1 181.0 %project_1.1 = (bf16[4,2,1024,256]{3,2,1,0:T(8,128)(2,1)}, bf16[4,2,4,1024,256]{4,3,2,1,0:T(8,128)(2,1)}, bf16[8,1024,256]{2,1,0:T(8,128)(2,1)}, bf16[1280,512]{1,0:T(8,128)(2,1)}, bf16[1,4,1280,512]{3,2,1,0:T(8,128)(2,1)}) custom-call(bf16[4,4,256,512]{3,2,1,0:T(8,128)(2,1)} %get-tuple-element.35.refs_0_.refs_4_, ...), custom_call_target="tpu_custom_call" | custom-call | flops 77309411328 | bytes 33554432 | tf_op jit(solution)/shard_map/project_1/pallas_call | solution.py:569
  552.1 135.9 %attend_and_sum_1.1 = bf16[1024,2048]{1,0:T(8,128)(2,1)} custom-call(s32[8]{0:T(128)} %refs_0_.3, bf16[4,2,1024,256]{3,2,1,0:T(8,128)(2,1)} %get-tuple-element.40.refs_1_, bf16[4,2,4,1024,256]{4,3,2,1,0:T(8,128)(2,1)} %get-tuple-element.41.refs_2_, bf16[8,1024,256]{2,1,0:T(8,128)(2,1)} %get-tuple-element.42.refs_3_, ...), custom_call_target="tpu_custom_call" | custom-call | flops 42949672960 | bytes 33554432 | tf_op jit(solution)/shard_map/attend_and_sum_1/pallas_call | solution.py:911
  688.0 4.8 copy.8
